TPU v7x, 32 devices: a whole 2x2x4 slice. The times are simulated.
32 devices in a mesh: pipe: 1, seq: 32 (over z, y, x, core).
Axes of the slice: x: 2, y: 2, z: 4, core: 2. Of those that a mesh axis runs over, the one named last changes fastest.
Arguments:
- inputs: bfloat16 [2, 16384, 512], P(None, 'seq'), may hold values from -6 to 6
- w_in: bfloat16 [1, 512, 2048], P('pipe'), may hold values from -0.25 to 0.25
- w_out: bfloat16 [1, 512, 512], P('pipe'), may hold values from -0.25 to 0.25
- lengths: int32 [2, 8], replicated, may hold values from 1 to 4096, 16384 in all within a row
- valid: int32 [2, 32], replicated, may hold values from 128 to 512
Outputs:
- states: bfloat16 [1, 2, 16384, 512], P('pipe', None, 'seq')
Inputs may be any that keep to these rules, and one draw needn't show every extreme that they name: Each row of stream lengths sums to 16384.
All inputs are finite; a program needn't handle non-finite values.
Results may differ from a plain program's by a relative error of at most 0.025.
Values may be sent and summed in bfloat16 or wider, within the bound.
No kernel may reach another device: no remote copies, remote signals or barrier semaphores. Data moves between devices by JAX's collectives and lax.ppermute only.
A program may use at most 64 MiB of HBM per device.

v0:
```python
import math

import jax
import jax.numpy as jnp
from jax import lax
from jax.sharding import PartitionSpec as P

HEAD_DIM = 128
WINDOW = 512


norm_eps = 1e-05
out_eps = 0.001


def shifted(x, axis, by):
    size = lax.axis_size(axis)
    pairs = [(i, i + by) for i in range(size) if 0 <= i + by < size]
    return lax.ppermute(x, axis, pairs)


def layer_norm(values, epsilon):
    mean = jnp.mean(values, axis=-1, keepdims=True)
    centred = values - mean
    spread = jnp.mean(centred * centred, axis=-1, keepdims=True)
    return centred * lax.rsqrt(spread + epsilon)


def shards(inputs, w_in, w_out, lengths, valid):
    micro = inputs.shape[0]
    tok = inputs.shape[1]
    width = inputs.shape[2]
    branch_width = w_out.shape[1]
    heads = branch_width // HEAD_DIM
    groups = valid.shape[1]
    sections = lax.axis_size("pipe")
    section = lax.axis_index("pipe")
    block_index = lax.axis_index("seq")
    key_rows = WINDOW + tok
    wide_in = w_in[0]
    wide_out = w_out[0]
    kv_weight = jnp.concatenate(
        [wide_in[:, 3 * branch_width :], wide_in[:, branch_width : 2 * branch_width]], 1
    )
    score_scale = 1.0 / math.sqrt(HEAD_DIM)
    mix_scale = 1.0 / math.sqrt(WINDOW)
    key_pos = block_index * tok - WINDOW + jnp.arange(key_rows, dtype=jnp.int32)
    query_pos = key_pos[WINDOW:]
    key_block = jnp.floor_divide(key_pos, tok)
    group_ids = jnp.arange(groups, dtype=jnp.int32)

    def project(x_rows):
        normed = layer_norm(x_rows.astype(jnp.float32), norm_eps).astype(jnp.bfloat16)
        proj = jax.nn.silu(jnp.dot(normed, wide_in, preferred_element_type=jnp.float32)).astype(
            jnp.bfloat16
        )
        return (normed, proj)

    def project_spare(x_rows):
        return (
            jnp.zeros((tok, width), jnp.bfloat16),
            jnp.zeros((tok, 4 * branch_width), jnp.bfloat16),
        )

    def tick(step, carry):
        incoming, states = carry
        slot = step - section
        active = (slot >= 0) & (slot < micro)
        index = jnp.clip(slot, 0, micro - 1)
        fresh = lax.dynamic_index_in_dim(inputs, index, 0, keepdims=False)
        x_rows = jnp.where(section == 0, fresh, incoming)
        bounds = jnp.cumsum(lax.dynamic_index_in_dim(lengths, index, 0, keepdims=False))
        valid_row = lax.dynamic_index_in_dim(valid, index, 0, keepdims=False)
        counts = jnp.sum(
            jnp.where(key_block[:, None] == group_ids[None, :], valid_row[None, :], 0), axis=1
        )
        key_live = (key_pos >= 0) & (jnp.mod(key_pos, tok) < counts)
        key_stream = jnp.sum((key_pos[:, None] >= bounds[None, :]).astype(jnp.int32), axis=1)
        query_live = key_live[WINDOW:]
        query_stream = key_stream[WINDOW:]
        allowed = (
            query_live[:, None]
            & key_live[None, :]
            & (query_stream[:, None] == key_stream[None, :])
            & (key_pos[None, :] <= query_pos[:, None])
            & (query_pos[:, None] - key_pos[None, :] < WINDOW)
        )
        normed, proj = lax.cond(active, project, project_spare, x_rows)
        own_kv = jnp.concatenate(
            [proj[:, 3 * branch_width :], proj[:, branch_width : 2 * branch_width]], 1
        )
        pieces = [shifted(normed, "seq", 1)]
        received = jnp.concatenate(pieces, 0)

        def finish(x_rows):
            remote_kv = jax.nn.silu(
                jnp.dot(received, kv_weight, preferred_element_type=jnp.float32)
            ).astype(jnp.bfloat16)
            all_kv = jnp.concatenate([remote_kv, own_kv], 0)
            keys = all_kv[:, :branch_width].reshape(key_rows, heads, HEAD_DIM)
            values = all_kv[:, branch_width:].reshape(key_rows, heads, HEAD_DIM)
            query = proj[:, 2 * branch_width : 3 * branch_width].reshape(tok, heads, HEAD_DIM)
            scores = jnp.einsum("qhd,khd->hqk", query, keys, preferred_element_type=jnp.float32)
            weights = jnp.where(
                allowed[None], jax.nn.silu(scores * score_scale) * mix_scale, 0.0
            ).astype(jnp.bfloat16)
            attended = jnp.einsum(
                "hqk,khd->qhd", weights, values, preferred_element_type=jnp.float32
            ).reshape(tok, branch_width)
            gated = (
                layer_norm(attended, out_eps) * proj[:, :branch_width].astype(jnp.float32)
            ).astype(jnp.bfloat16)
            return (
                x_rows.astype(jnp.float32)
                + jnp.dot(gated, wide_out, preferred_element_type=jnp.float32)
            ).astype(jnp.bfloat16)

        def finish_spare(x_rows):
            return x_rows

        result = lax.cond(active, finish, finish_spare, x_rows)
        zero_index = jnp.zeros((), jnp.int32)
        updated = lax.dynamic_update_slice(
            states, result[None, None], (zero_index, index, zero_index, zero_index)
        )
        states = jnp.where(active, updated, states)
        incoming = shifted(result, "pipe", 1)
        return (incoming, states)

    start_states = jnp.zeros((1, micro, tok, width), jnp.bfloat16)
    start_rows = jnp.zeros((tok, width), jnp.bfloat16)
    final_rows, states = lax.fori_loop(0, sections + micro - 1, tick, (start_rows, start_states))
    return states


def solution(mesh):
    in_specs = (P(None, "seq", None), P("pipe", None, None), P("pipe", None, None), P(), P())
    out_specs = P("pipe", None, "seq", None)
    return jax.shard_map(shards, mesh=mesh, in_specs=in_specs, out_specs=out_specs, check_vma=False)
```

profile of v0, /device:TPU:16, one launch (start us, length us, event | category | flops | bytes accessed | tf_op | source)
XLA Modules:
  0.0 80.6 jit_solution(15296870078246308361)
XLA Ops:
  0.0 1.3 %fusion.56 = (bf16[512,512]{1,0:T(8,128)(2,1)S(1)}, bf16[512,512]{1,0:T(8,128)(2,1)S(1)}) fusion(bf16[512,2048]{1,0:T(8,128)(2,1)} %bitcast.92), kind=kLoop, calls=%fused_computation.83 | loop fusion | bytes 2097152 | tf_op jit(solution)/shard_map/slice | solution.py:43
  1.3 0.0 copy-start.3
  1.3 0.0 copy-start.4
  1.3 1.1 %pad_maximum_fusion.2 = bf16[512,1024]{1,0:T(8,128)(2,1)} fusion(bf16[512,512]{1,0:T(8,128)(2,1)S(1)} %get-tuple-element.1019, bf16[512,512]{1,0:T(8,128)(2,1)S(1)} %get-tuple-element.1018), kind=kLoop, calls=%fused_computation.79 | loop fusion | flops 2097152 | bytes 2097152 | tf_op jit(solution)/shard_map/concatenate | solution.py:42
  2.4 1.0 %broadcast_in_dim.124 = bf16[1,2,512,512]{3,2,1,0:T(8,128)(2,1)} broadcast(bf16[]{:T(256)} %constant.163.clone.1), dimensions={} | broadcast | bytes 1048578 | tf_op jit(solution)/shard_map/broadcast_in_dim | solution.py:130
  3.5 0.0 copy-done.4
  3.5 77.1 %while.20 = (s32[]{:T(128)}, bf16[1,2,512,512]{3,2,1,0:T(8,128)(2,1)}, bf16[2,512,512]{2,1,0:T(8,128)(2,1)}, bf16[512,2048]{1,0:T(8,128)(2,1)}, s32[2,8]{1,0:T(2...) while((s32[]{:T(128)}, ...), condition=%wide.region_12.13_spmd.clone.clone, body=%wide.region_0.12_spmd.clone.clone.sunk | while | flops 2994118656 | bytes 54770072 | solution.py:132
  3.5 1.1 %dynamic-slice_bitcast_fusion.3 = bf16[512,512]{1,0:T(8,128)(2,1)S(1)} fusion(bf16[2,512,512]{2,1,0:T(8,128)(2,1)} %get-tuple-element.1133, s32[]{:T(128)} %min.16), kind=kLoop, calls=%fused_computation.69.clone.1 | loop fusion | bytes 1048580 | tf_op jit(solution)/shard_map/while/body/eval_jaxpr/jit(dynamic_index_in_dim)/squeeze | solution.py:70
  4.6 4.3 %conditional.8 = (bf16[512,512]{1,0:T(8,128)(2,1)}, bf16[512,2048]{1,0:T(8,128)(2,1)S(1)}) conditional(s32[]{:T(128)} %convert_element_type.107, () %tuple.150, (bf16[512,512]{1,0:T(8,128)(2,1)S(1)}, bf16[512,2048]{1,0:T(8,128)(2,1)}) %tuple.151), branch_computations={%region_1.1_spmd, %region_2.4_spmd} | conditional | flops 1081606656 | bytes 15222828 | solution.py:88
  4.6 0.0 copy-start.1
  4.6 0.1 convert_reduce_fusion
  4.7 0.3 fusion.12
  5.1 1.0 %fusion.13 = bf16[512,512]{1,0:T(8,128)(2,1)} fusion(bf16[512,512]{1,0:T(8,128)(2,1)S(1)} %get-tuple-element.657, f32[512]{0:T(512)S(1)} %add_rsqrt_fusion, f32[512]{0:T(512)S(1)} %broadcast_multiply_fusion), kind=kLoop, calls=%fused_computation.11 | loop fusion | flops 1048576 | bytes 1052672 | tf_op jit(solution)/shard_map/while/body/eval_jaxpr/cond/branch_1_fun/convert_element_type | solution.py:53
  6.1 0.1 copy-done.1
  6.2 2.7 %multiply_convert_fusion = bf16[512,2048]{1,0:T(8,128)(2,1)S(1)} fusion(bf16[512,512]{1,0:T(8,128)(2,1)} %fusion.13, bf16[512,2048]{1,0:T(8,128)(2,1)S(1)} %copy-done.1), kind=kOutput, calls=%fused_computation.5 | convolution fusion | flops 1078984704 | bytes 4718592 | tf_op jit(solution)/shard_map/while/body/eval_jaxpr/cond/branch_1_fun/dot_general | solution.py:54
  8.9 1.9 %collective-permute-start = (bf16[512,512]{1,0:T(8,128)(2,1)}, bf16[512,512]{1,0:T(8,128)(2,1)}, u32[]{:S(2)}, u32[]{:S(2)}) collective-permute-start(bf16[512,512]{1,0:T(8,128)(2,1)} %get-tuple-element.1090), channel_id=1, source_target_pairs={{0,1},{1,2},{2,3},{3,4},{4,5},{5,6},{6,7},{7,8},{8,9},{9,10},{10,1... | collective-permute-start | bytes 1572872 | tf_op jit(solution)/shard_map/while/body/eval_jaxpr/ppermute | solution.py:19
  10.8 0.9 %fusion.69 = (bf16[512,512]{1,0:T(8,128)(2,1)S(1)}, bf16[512,512]{1,0:T(8,128)(2,1)}) fusion(bf16[512,2048]{1,0:T(8,128)(2,1)S(1)} %get-tuple-element.1162), kind=kLoop, calls=%fused_computation.82.clone.1 | loop fusion | bytes 2097152 | tf_op jit(solution)/shard_map/while/body/eval_jaxpr/slice | solution.py:90
  11.7 0.2 reduce-window.15
  11.9 2.1 %pad_maximum_fusion.4 = bf16[512,1024]{1,0:T(8,128)(2,1)} fusion(bf16[512,512]{1,0:T(8,128)(2,1)} %get-tuple-element.1092, bf16[512,512]{1,0:T(8,128)(2,1)S(1)} %get-tuple-element.1093), kind=kLoop, calls=%fused_computation.67.clone.1 | loop fusion | flops 2097152 | bytes 2097152 | tf_op jit(solution)/shard_map/while/body/eval_jaxpr/concatenate | solution.py:89
  14.1 0.1 compare_convert_fusion.2
  14.1 7.4 %collective-permute-done = bf16[512,512]{1,0:T(8,128)(2,1)} collective-permute-done((bf16[512,512]{1,0:T(8,128)(2,1)}, bf16[512,512]{1,0:T(8,128)(2,1)}, u32[]{:S(2)}, u32[]{:S(2)}) %collective-permute-start) | collective-permute-done | bytes 524320 | tf_op jit(solution)/shard_map/while/body/eval_jaxpr/ppermute | solution.py:19
  21.5 18.5 %conditional.9 = (bf16[1,1,512,512]{3,2,1,0:T(8,128)(2,1)S(1)}) conditional(s32[]{:T(128)} %convert_element_type.107, bf16[512,512]{1,0:T(8,128)(2,1)S(1)} %dynamic-slice_bitcast_fusion.3, (bf16[512,512]{1,0:T(8,128)(2,1)S(1)}, bf16[512,512]{1,0:T(8,128)(2,1)}, bf16[512,1024]{1,0:T(8,128)(2,1)}, bf16[512,1024]{1,0:T(8,128)(2,1)}, ...), branch_computations={%region_6.6_spmd, %region_7.11_spmd.clone.clone} | conditional | flops 1910121984 | bytes 30566488 | solution.py:121
  21.6 0.1 select_reduce_fusion
  21.8 1.2 %fusion.24 = pred[512,1024]{0,1:T(8,128)(4,1)S(1)} fusion(s32[512]{0:T(512)S(1)} %get-tuple-element.939, s32[512]{0:T(512)S(1)} %slice.90, s32[1024]{0:T(1024)S(1)} %bitcast.90, s32[1024]{0:T(1024)S(1)} %reduce_sum.88, pred[512]{0:T(512)(128)(4,1)S(1)} %slice.89, pred[1024]{0:T(1024)(128)(4,1)S(1)} %and_reduce_fusion), kind=kLoop, calls=%fused_computation.28 | loop fusion | flops 4194304 | bytes 538112 | tf_op jit(solution)/shard_map/while/body/eval_jaxpr/and | solution.py:82
  23.0 2.4 %multiply_convert_fusion.1 = bf16[512,1024]{1,0:T(8,128)(2,1)S(1)} fusion(bf16[512,512]{1,0:T(8,128)(2,1)} %get-tuple-element.926, bf16[512,1024]{1,0:T(8,128)(2,1)} %get-tuple-element.927), kind=kOutput, calls=%fused_computation.27 | convolution fusion | flops 539492352 | bytes 2621440 | tf_op jit(solution)/shard_map/while/body/eval_jaxpr/cond/branch_1_fun/dot_general | solution.py:97
  25.4 0.0 copy-done
  25.4 1.6 %fusion.32 = (bf16[128,4,8,128]{3,2,1,0:T(8,128)(2,1)}, bf16[1024,512]{1,0:T(8,128)(2,1)}) fusion(bf16[512,1024]{1,0:T(8,128)(2,1)S(1)} %copy-done, bf16[512,1024]{1,0:T(8,128)(2,1)S(1)} %multiply_convert_fusion.1), kind=kLoop, calls=%fused_computation.36 | loop fusion | flops 4194304 | bytes 4194304 | tf_op jit(solution)/shard_map/while/body/eval_jaxpr/cond
  27.0 2.3 %copy.25 = bf16[1024,512]{0,1:T(8,128)(2,1)} copy(bf16[1024,512]{1,0:T(8,128)(2,1)} %get-tuple-element.1009) | data formatting | bytes 2097152 | tf_op jit(solution)/shard_map/while/body/eval_jaxpr/cond/branch_1_fun/reshape | solution.py:101
  29.3 2.5 %copy.24 = bf16[512,2048]{0,1:T(8,128)(2,1)} copy(bf16[512,2048]{1,0:T(8,128)(2,1)S(1)} %get-tuple-element.940) | data formatting | bytes 4194304 | tf_op jit(solution)/shard_map
  31.8 1.1 %slice.96 = bf16[512,512]{0,1:T(8,128)(2,1)S(1)} slice(bf16[512,2048]{0,1:T(8,128)(2,1)} %copy.24), slice={[0:512], [1024:1536]} | slice | bytes 1048576 | tf_op jit(solution)/shard_map/while/body/eval_jaxpr/cond/branch_1_fun/slice | solution.py:102
  32.8 5.2 %fusion.52 = (f32[512]{0:T(512)S(1)}, f32[4,128,512]{2,1,0:T(8,128)S(1)}) fusion(bf16[1024,4,128]{0,2,1:T(8,128)(2,1)} %bitcast.84, pred[512,1024]{0,1:T(8,128)(4,1)S(1)} %fusion.24, bf16[512,4,128]{0,2,1:T(8,128)(2,1)S(1)} %bitcast.85, bf16[128,4,8,128]{3,2,1,0:T(8,128)(2,1)} %get-tuple-element.1008), kind=kOutput, calls=%fused_computation.81 | convolution fusion | flops 1090780672 | bytes 4196352 | tf_op jit(solution)/shard_map/while/body/eval_jaxpr/cond/branch_1_fun/hqk,khd->qhd/dot_general | solution.py:107
  38.1 0.0 copy-start.2
  38.1 0.2 fusion.37
  38.3 1.3 %fusion.35 = bf16[512,512]{0,1:T(8,128)(2,1)S(1)} fusion(f32[4,128,512]{2,1,0:T(8,128)S(1)} %get-tuple-element.1011, bf16[512,2048]{0,1:T(8,128)(2,1)} %copy.24, f32[512]{0:T(512)S(1)} %add_rsqrt_fusion.1, f32[512]{0:T(512)S(1)} %broadcast_multiply_fusion.1), kind=kLoop, calls=%fused_computation.40 | loop fusion | flops 1310720 | bytes 2101248 | tf_op jit(solution)/shard_map/while/body/eval_jaxpr/cond/branch_1_fun/convert_element_type | solution.py:112
  39.6 0.5 fusion.26
  40.1 2.0 %select_dynamic-update-slice_fusion.2 = bf16[1,2,512,512]{3,2,1,0:T(8,128)(2,1)} fusion(bf16[1,2,512,512]{3,2,1,0:T(8,128)(2,1)} %get-tuple-element.1119, s32[]{:T(128)} %min.16, bf16[1,1,512,512]{3,2,1,0:T(8,128)(2,1)S(1)} %get-tuple-element.1098, pred[]{:T(512)S(6)} %ge.107), kind=kLoop, calls=%fused_computation.68.clone.1 | loop fusion | flops 262144 | bytes 1573377 | tf_op jit(solution)/shard_map/while/body/eval_jaxpr/jit(_where)/select_n | solution.py:126
  42.0 1.1 %dynamic-slice_bitcast_fusion.3 = bf16[512,512]{1,0:T(8,128)(2,1)S(1)} fusion(bf16[2,512,512]{2,1,0:T(8,128)(2,1)} %get-tuple-element.1133, s32[]{:T(128)} %min.16), kind=kLoop, calls=%fused_computation.69.clone.1 | loop fusion | bytes 1048580 | tf_op jit(solution)/shard_map/while/body/eval_jaxpr/jit(dynamic_index_in_dim)/squeeze | solution.py:70
  43.1 4.3 %conditional.8 = (bf16[512,512]{1,0:T(8,128)(2,1)}, bf16[512,2048]{1,0:T(8,128)(2,1)S(1)}) conditional(s32[]{:T(128)} %convert_element_type.107, () %tuple.150, (bf16[512,512]{1,0:T(8,128)(2,1)S(1)}, bf16[512,2048]{1,0:T(8,128)(2,1)}) %tuple.151), branch_computations={%region_1.1_spmd, %region_2.4_spmd} | conditional | flops 1081606656 | bytes 15222828 | solution.py:88
  43.1 0.0 copy-start.1
  43.1 0.1 convert_reduce_fusion
  43.3 0.3 fusion.12
  43.6 1.0 %fusion.13 = bf16[512,512]{1,0:T(8,128)(2,1)} fusion(bf16[512,512]{1,0:T(8,128)(2,1)S(1)} %get-tuple-element.657, f32[512]{0:T(512)S(1)} %add_rsqrt_fusion, f32[512]{0:T(512)S(1)} %broadcast_multiply_fusion), kind=kLoop, calls=%fused_computation.11 | loop fusion | flops 1048576 | bytes 1052672 | tf_op jit(solution)/shard_map/while/body/eval_jaxpr/cond/branch_1_fun/convert_element_type | solution.py:53
  44.6 0.1 copy-done.1
  44.7 2.7 %multiply_convert_fusion = bf16[512,2048]{1,0:T(8,128)(2,1)S(1)} fusion(bf16[512,512]{1,0:T(8,128)(2,1)} %fusion.13, bf16[512,2048]{1,0:T(8,128)(2,1)S(1)} %copy-done.1), kind=kOutput, calls=%fused_computation.5 | convolution fusion | flops 1078984704 | bytes 4718592 | tf_op jit(solution)/shard_map/while/body/eval_jaxpr/cond/branch_1_fun/dot_general | solution.py:54
  47.4 1.9 %collective-permute-start = (bf16[512,512]{1,0:T(8,128)(2,1)}, bf16[512,512]{1,0:T(8,128)(2,1)}, u32[]{:S(2)}, u32[]{:S(2)}) collective-permute-start(bf16[512,512]{1,0:T(8,128)(2,1)} %get-tuple-element.1090), channel_id=1, source_target_pairs={{0,1},{1,2},{2,3},{3,4},{4,5},{5,6},{6,7},{7,8},{8,9},{9,10},{10,1... | collective-permute-start | bytes 1572872 | tf_op jit(solution)/shard_map/while/body/eval_jaxpr/ppermute | solution.py:19
  49.4 0.9 %fusion.69 = (bf16[512,512]{1,0:T(8,128)(2,1)S(1)}, bf16[512,512]{1,0:T(8,128)(2,1)}) fusion(bf16[512,2048]{1,0:T(8,128)(2,1)S(1)} %get-tuple-element.1162), kind=kLoop, calls=%fused_computation.82.clone.1 | loop fusion | bytes 2097152 | tf_op jit(solution)/shard_map/while/body/eval_jaxpr/slice | solution.py:90
  50.3 0.2 reduce-window.15
  50.5 2.1 %pad_maximum_fusion.4 = bf16[512,1024]{1,0:T(8,128)(2,1)} fusion(bf16[512,512]{1,0:T(8,128)(2,1)} %get-tuple-element.1092, bf16[512,512]{1,0:T(8,128)(2,1)S(1)} %get-tuple-element.1093), kind=kLoop, calls=%fused_computation.67.clone.1 | loop fusion | flops 2097152 | bytes 2097152 | tf_op jit(solution)/shard_map/while/body/eval_jaxpr/concatenate | solution.py:89
  52.6 0.1 compare_convert_fusion.2
  52.7 7.4 %collective-permute-done = bf16[512,512]{1,0:T(8,128)(2,1)} collective-permute-done((bf16[512,512]{1,0:T(8,128)(2,1)}, bf16[512,512]{1,0:T(8,128)(2,1)}, u32[]{:S(2)}, u32[]{:S(2)}) %collective-permute-start) | collective-permute-done | bytes 524320 | tf_op jit(solution)/shard_map/while/body/eval_jaxpr/ppermute | solution.py:19
  60.1 18.5 %conditional.9 = (bf16[1,1,512,512]{3,2,1,0:T(8,128)(2,1)S(1)}) conditional(s32[]{:T(128)} %convert_element_type.107, bf16[512,512]{1,0:T(8,128)(2,1)S(1)} %dynamic-slice_bitcast_fusion.3, (bf16[512,512]{1,0:T(8,128)(2,1)S(1)}, bf16[512,512]{1,0:T(8,128)(2,1)}, bf16[512,1024]{1,0:T(8,128)(2,1)}, bf16[512,1024]{1,0:T(8,128)(2,1)}, ...), branch_computations={%region_6.6_spmd, %region_7.11_spmd.clone.clone} | conditional | flops 1910121984 | bytes 30566488 | solution.py:121
  60.2 0.1 select_reduce_fusion
  60.4 1.2 %fusion.24 = pred[512,1024]{0,1:T(8,128)(4,1)S(1)} fusion(s32[512]{0:T(512)S(1)} %get-tuple-element.939, s32[512]{0:T(512)S(1)} %slice.90, s32[1024]{0:T(1024)S(1)} %bitcast.90, s32[1024]{0:T(1024)S(1)} %reduce_sum.88, pred[512]{0:T(512)(128)(4,1)S(1)} %slice.89, pred[1024]{0:T(1024)(128)(4,1)S(1)} %and_reduce_fusion), kind=kLoop, calls=%fused_computation.28 | loop fusion | flops 4194304 | bytes 538112 | tf_op jit(solution)/shard_map/while/body/eval_jaxpr/and | solution.py:82
  61.5 2.4 %multiply_convert_fusion.1 = bf16[512,1024]{1,0:T(8,128)(2,1)S(1)} fusion(bf16[512,512]{1,0:T(8,128)(2,1)} %get-tuple-element.926, bf16[512,1024]{1,0:T(8,128)(2,1)} %get-tuple-element.927), kind=kOutput, calls=%fused_computation.27 | convolution fusion | flops 539492352 | bytes 2621440 | tf_op jit(solution)/shard_map/while/body/eval_jaxpr/cond/branch_1_fun/dot_general | solution.py:97
  64.0 1.6 %fusion.32 = (bf16[128,4,8,128]{3,2,1,0:T(8,128)(2,1)}, bf16[1024,512]{1,0:T(8,128)(2,1)}) fusion(bf16[512,1024]{1,0:T(8,128)(2,1)S(1)} %copy-done, bf16[512,1024]{1,0:T(8,128)(2,1)S(1)} %multiply_convert_fusion.1), kind=kLoop, calls=%fused_computation.36 | loop fusion | flops 4194304 | bytes 4194304 | tf_op jit(solution)/shard_map/while/body/eval_jaxpr/cond
  65.5 2.3 %copy.25 = bf16[1024,512]{0,1:T(8,128)(2,1)} copy(bf16[1024,512]{1,0:T(8,128)(2,1)} %get-tuple-element.1009) | data formatting | bytes 2097152 | tf_op jit(solution)/shard_map/while/body/eval_jaxpr/cond/branch_1_fun/reshape | solution.py:101
  67.8 2.5 %copy.24 = bf16[512,2048]{0,1:T(8,128)(2,1)} copy(bf16[512,2048]{1,0:T(8,128)(2,1)S(1)} %get-tuple-element.940) | data formatting | bytes 4194304 | tf_op jit(solution)/shard_map
  70.3 1.1 %slice.96 = bf16[512,512]{0,1:T(8,128)(2,1)S(1)} slice(bf16[512,2048]{0,1:T(8,128)(2,1)} %copy.24), slice={[0:512], [1024:1536]} | slice | bytes 1048576 | tf_op jit(solution)/shard_map/while/body/eval_jaxpr/cond/branch_1_fun/slice | solution.py:102
  71.4 5.2 %fusion.52 = (f32[512]{0:T(512)S(1)}, f32[4,128,512]{2,1,0:T(8,128)S(1)}) fusion(bf16[1024,4,128]{0,2,1:T(8,128)(2,1)} %bitcast.84, pred[512,1024]{0,1:T(8,128)(4,1)S(1)} %fusion.24, bf16[512,4,128]{0,2,1:T(8,128)(2,1)S(1)} %bitcast.85, bf16[128,4,8,128]{3,2,1,0:T(8,128)(2,1)} %get-tuple-element.1008), kind=kOutput, calls=%fused_computation.81 | convolution fusion | flops 1090780672 | bytes 4196352 | tf_op jit(solution)/shard_map/while/body/eval_jaxpr/cond/branch_1_fun/hqk,khd->qhd/dot_general | solution.py:107
  76.6 0.0 copy-start.2
  76.6 0.2 fusion.37
  76.8 1.3 %fusion.35 = bf16[512,512]{0,1:T(8,128)(2,1)S(1)} fusion(f32[4,128,512]{2,1,0:T(8,128)S(1)} %get-tuple-element.1011, bf16[512,2048]{0,1:T(8,128)(2,1)} %copy.24, f32[512]{0:T(512)S(1)} %add_rsqrt_fusion.1, f32[512]{0:T(512)S(1)} %broadcast_multiply_fusion.1), kind=kLoop, calls=%fused_computation.40 | loop fusion | flops 1310720 | bytes 2101248 | tf_op jit(solution)/shard_map/while/body/eval_jaxpr/cond/branch_1_fun/convert_element_type | solution.py:112
  78.1 0.5 fusion.26
  78.6 2.0 %select_dynamic-update-slice_fusion.2 = bf16[1,2,512,512]{3,2,1,0:T(8,128)(2,1)} fusion(bf16[1,2,512,512]{3,2,1,0:T(8,128)(2,1)} %get-tuple-element.1119, s32[]{:T(128)} %min.16, bf16[1,1,512,512]{3,2,1,0:T(8,128)(2,1)S(1)} %get-tuple-element.1098, pred[]{:T(512)S(6)} %ge.107), kind=kLoop, calls=%fused_computation.68.clone.1 | loop fusion | flops 262144 | bytes 1573377 | tf_op jit(solution)/shard_map/while/body/eval_jaxpr/jit(_where)/select_n | solution.py:126
  (46 shorter events, 0.4 us)
Async XLA Ops:
  1.3 2.2 %copy-start.3 = (s32[2,8]{1,0:T(2,128)S(1)}, s32[2,8]{1,0:T(2,128)}, u32[]{:S(2)}) copy-start(s32[2,8]{1,0:T(2,128)} %param.14) | copy-start | bytes 196
  1.3 2.2 %copy-start.4 = (s32[2,32]{1,0:T(2,128)S(1)}, s32[2,32]{1,0:T(2,128)}, u32[]{:S(2)}) copy-start(s32[2,32]{1,0:T(2,128)} %param.15) | copy-start | bytes 772
  4.6 1.6 %copy-start.1 = (bf16[512,2048]{1,0:T(8,128)(2,1)S(1)}, bf16[512,2048]{1,0:T(8,128)(2,1)}, u32[]{:S(2)}) copy-start(bf16[512,2048]{1,0:T(8,128)(2,1)} %get-tuple-element.658) | copy-start | bytes 6291460 | tf_op jit(solution)/shard_map/while/body/eval_jaxpr/cond
  8.9 12.6 %collective-permute-start = (bf16[512,512]{1,0:T(8,128)(2,1)}, bf16[512,512]{1,0:T(8,128)(2,1)}, u32[]{:S(2)}, u32[]{:S(2)}) collective-permute-start(bf16[512,512]{1,0:T(8,128)(2,1)} %get-tuple-element.1090), channel_id=1, source_target_pairs={{0,1},{1,2},{2,3},{3,4},{4,5},{5,6},{6,7},{7,8},{8,9},{9,10},{10,1... | collective-permute-start | bytes 1572872 | tf_op jit(solution)/shard_map/while/body/eval_jaxpr/ppermute | solution.py:19
  23.0 2.4 %copy-start = (bf16[512,1024]{1,0:T(8,128)(2,1)S(1)}, bf16[512,1024]{1,0:T(8,128)(2,1)}, u32[]{:S(2)}) copy-start(bf16[512,1024]{1,0:T(8,128)(2,1)} %get-tuple-element.928) | copy-start | bytes 3145732 | tf_op jit(solution)/shard_map/while/body/eval_jaxpr/cond
  38.1 1.5 %copy-start.2 = (bf16[512,512]{1,0:T(8,128)(2,1)S(1)}, bf16[512,512]{1,0:T(8,128)(2,1)}, u32[]{:S(2)}) copy-start(bf16[512,512]{1,0:T(8,128)(2,1)} %get-tuple-element.941) | copy-start | bytes 1572868 | tf_op jit(solution)/shard_map/while/body/eval_jaxpr/cond
  43.1 1.6 %copy-start.1 = (bf16[512,2048]{1,0:T(8,128)(2,1)S(1)}, bf16[512,2048]{1,0:T(8,128)(2,1)}, u32[]{:S(2)}) copy-start(bf16[512,2048]{1,0:T(8,128)(2,1)} %get-tuple-element.658) | copy-start | bytes 6291460 | tf_op jit(solution)/shard_map/while/body/eval_jaxpr/cond
  47.4 12.6 %collective-permute-start = (bf16[512,512]{1,0:T(8,128)(2,1)}, bf16[512,512]{1,0:T(8,128)(2,1)}, u32[]{:S(2)}, u32[]{:S(2)}) collective-permute-start(bf16[512,512]{1,0:T(8,128)(2,1)} %get-tuple-element.1090), channel_id=1, source_target_pairs={{0,1},{1,2},{2,3},{3,4},{4,5},{5,6},{6,7},{7,8},{8,9},{9,10},{10,1... | collective-permute-start | bytes 1572872 | tf_op jit(solution)/shard_map/while/body/eval_jaxpr/ppermute | solution.py:19
  61.5 2.4 %copy-start = (bf16[512,1024]{1,0:T(8,128)(2,1)S(1)}, bf16[512,1024]{1,0:T(8,128)(2,1)}, u32[]{:S(2)}) copy-start(bf16[512,1024]{1,0:T(8,128)(2,1)} %get-tuple-element.928) | copy-start | bytes 3145732 | tf_op jit(solution)/shard_map/while/body/eval_jaxpr/cond
  76.6 1.5 %copy-start.2 = (bf16[512,512]{1,0:T(8,128)(2,1)S(1)}, bf16[512,512]{1,0:T(8,128)(2,1)}, u32[]{:S(2)}) copy-start(bf16[512,512]{1,0:T(8,128)(2,1)} %get-tuple-element.941) | copy-start | bytes 1572868 | tf_op jit(solution)/shard_map/while/body/eval_jaxpr/cond
where the time goes:
time: 81.5 us; the launch traced here: 80.6 us
  matrix products  21.7 us (27%)
  other arithmetic  21.6 us (27%)
  local copies, waits for them, and re-layouts  18.3 us (22%)
  waiting for transfers between devices  14.7 us (18%)
  starting transfers between devices  3.84 us (5%)
    ppermute x2, waiting for transfers between devices, shifted(): return lax.ppermute(x, axis, pairs)  14.7 us
    dot_general x2, matrix products, finish(): jnp.einsum('hqk,khd->qhd', weights, values, preferred_element_type=jnp.fl...  10.4 us
    dot_general x2, matrix products, project(): jnp.dot(normed, wide_in, preferred_element_type=jnp.float32)  5.43 us
    another operation x8, local copies, waits for them, and re-layouts  5.03 us
    dot_general x2, matrix products, finish(): jnp.dot(received, kv_weight, preferred_element_type=jnp.float32)  4.84 us
    reshape x2, local copies, waits for them, and re-layouts, finish(): values = all_kv[:, branch_width:].reshape(key_rows, heads, HEAD_DIM)  4.56 us
    concatenate x2, other arithmetic, tick(): jnp.concatenate([proj[:, 3 * branch_width:], proj[:, branch_width:2 * bra...  4.27 us
    select_n x2, other arithmetic, tick(): states = jnp.where(active, updated, states)  3.95 us
  transfers between devices with their start and end apart: 2, of which 2 were waited for; matrix products, arithmetic and copies ran while one was open for 8% of the time, Pallas kernels for 0%

commit v1 on v0

v1 whole, which is shorter than its diff:
```python
import functools
import math

import jax
import jax.numpy as jnp
from jax import lax
from jax.experimental import pallas as pl
from jax.experimental.pallas import tpu as pltpu
from jax.sharding import PartitionSpec as P

HEAD_DIM = 128
WINDOW = 512
TILE = 128
ROW_TILE = 256

norm_eps = 1e-05
out_eps = 0.001

FAR = 1 << 30


def shifted(x, axis, by):
    size = lax.axis_size(axis)
    pairs = [(i, i + by) for i in range(size) if 0 <= i + by < size]
    return lax.ppermute(x, axis, pairs)


def normalise(values, epsilon):
    mean = jnp.mean(values, axis=-1, keepdims=True)
    centred = values - mean
    spread = jnp.mean(centred * centred, axis=-1, keepdims=True)
    return centred * lax.rsqrt(spread + epsilon)


def half_silu(half):
    return half + half * jnp.tanh(half)


def stream_floor(lengths, slot, base, rows):
    place = base + lax.broadcasted_iota(jnp.int32, (rows, TILE), 0)
    bound = jnp.int32(0)
    start = jnp.zeros((rows, TILE), jnp.int32)
    for k in range(lengths.shape[1]):
        bound = bound + lengths[slot, k]
        start = jnp.where(place >= bound, bound, start)
    return start - base


def own_kernel(spot, lengths, valid, x, w_in, gates, queries, mixed, keys, values, *, micro):
    tok = x.shape[1]
    branch = w_in.shape[1] // 4
    heads = branch // HEAD_DIM
    scale = 0.5 / math.sqrt(HEAD_DIM)
    block = spot[0]

    def one(m, _):
        slot = spot[1] + m
        for r in range(0, tok, ROW_TILE):
            rows = pl.ds(r, ROW_TILE)
            normed = normalise(x[m, rows, :].astype(jnp.float32), norm_eps).astype(jnp.bfloat16)
            for part in range(4):
                half = 0.5 * jnp.dot(
                    normed,
                    w_in[:, part * branch : (part + 1) * branch],
                    preferred_element_type=jnp.float32,
                )
                out = half_silu(half).astype(jnp.bfloat16)
                if part == 0:
                    gates[m, rows, :] = out
                elif part == 1:
                    values[rows, :] = out
                elif part == 2:
                    queries[m, rows, :] = out
                else:
                    keys[rows, :] = out
        floor = stream_floor(lengths, slot, block * tok, tok)
        count = valid[slot, block]
        for t in range(0, tok, TILE):
            span = t + TILE
            row = t + lax.broadcasted_iota(jnp.int32, (TILE, span), 0)
            col = lax.broadcasted_iota(jnp.int32, (TILE, span), 1)
            low = jnp.concatenate([floor[t : t + TILE]] * (span // TILE), 1)
            allowed = (col <= row) & (col >= low) & (row < count)
            for h in range(heads):
                lanes = slice(h * HEAD_DIM, (h + 1) * HEAD_DIM)
                half = scale * lax.dot_general(
                    queries[m, t : t + TILE, lanes],
                    keys[0:span, lanes],
                    (((1,), (1,)), ((), ())),
                    preferred_element_type=jnp.float32,
                )
                weights = jnp.where(allowed, half_silu(half), 0.0).astype(jnp.bfloat16)
                mixed[m, t : t + TILE, lanes] = jnp.dot(
                    weights, values[0:span, lanes], preferred_element_type=jnp.float32
                )
        return 0

    lax.fori_loop(0, micro, one, 0)


def far_kernel(
    spot, lengths, valid, before, x, w_in, w_out, gates, queries, mixed, *rest, offset
):
    out, keys, values = rest[-3:]
    tok = x.shape[1]
    branch = w_out.shape[0]
    heads = branch // HEAD_DIM
    scale = 0.5 / math.sqrt(HEAD_DIM)
    block = spot[0]
    slot = spot[1] + offset
    m = offset
    for r in range(0, tok, ROW_TILE):
        rows = pl.ds(r, ROW_TILE)
        normed = normalise(before[rows, :].astype(jnp.float32), norm_eps).astype(jnp.bfloat16)
        for part, kept in ((1, values), (3, keys)):
            half = 0.5 * jnp.dot(
                normed,
                w_in[:, part * branch : (part + 1) * branch],
                preferred_element_type=jnp.float32,
            )
            kept[rows, :] = half_silu(half).astype(jnp.bfloat16)
    floor = stream_floor(lengths, slot, block * tok, tok)
    count = valid[slot, block]
    count_before = valid[slot, jnp.maximum(block - 1, 0)]
    for t in range(tok - TILE, -1, -TILE):
        span = tok - t
        row = t + lax.broadcasted_iota(jnp.int32, (TILE, span), 0)
        col = t + lax.broadcasted_iota(jnp.int32, (TILE, span), 1)
        low = jnp.concatenate([floor[t : t + TILE]] * (span // TILE), 1) + tok
        allowed = (col > row) & (col >= low) & (col < count_before) & (row < count)
        parts = []
        for h in range(heads):
            lanes = slice(h * HEAD_DIM, (h + 1) * HEAD_DIM)
            half = scale * lax.dot_general(
                queries[m, t : t + TILE, lanes],
                keys[t:tok, lanes],
                (((1,), (1,)), ((), ())),
                preferred_element_type=jnp.float32,
            )
            weights = jnp.where(allowed, half_silu(half), 0.0).astype(jnp.bfloat16)
            parts.append(
                mixed[m, t : t + TILE, lanes]
                + jnp.dot(weights, values[t:tok, lanes], preferred_element_type=jnp.float32)
            )
        attended = normalise(jnp.concatenate(parts, 1), out_eps * WINDOW)
        gated = (attended * gates[m, t : t + TILE, :].astype(jnp.float32)).astype(jnp.bfloat16)
        out[0, 0, t : t + TILE, :] = (
            x[m, t : t + TILE, :].astype(jnp.float32)
            + jnp.dot(gated, w_out[...], preferred_element_type=jnp.float32)
        ).astype(jnp.bfloat16)


SMEM = pl.BlockSpec(memory_space=pltpu.SMEM)
VMEM = pl.BlockSpec(memory_space=pltpu.VMEM)
ANY = pl.BlockSpec(memory_space=pl.ANY)


def layer(x, w_in, w_out, lengths, valid, slot):
    micro, tok, width = x.shape
    branch = w_out.shape[0]
    spot = jnp.stack([lax.axis_index("seq").astype(jnp.int32), slot])
    arrived = [shifted(x[m], "seq", 1) for m in range(micro)]
    gates, queries, mixed = pl.pallas_call(
        functools.partial(own_kernel, micro=micro),
        out_shape=(
            jax.ShapeDtypeStruct((micro, tok, branch), jnp.bfloat16),
            jax.ShapeDtypeStruct((micro, tok, branch), jnp.bfloat16),
            jax.ShapeDtypeStruct((micro, tok, branch), jnp.float32),
        ),
        in_specs=[SMEM, SMEM, SMEM, VMEM, VMEM],
        out_specs=(VMEM, VMEM, VMEM),
        scratch_shapes=[
            pltpu.VMEM((tok, branch), jnp.bfloat16),
            pltpu.VMEM((tok, branch), jnp.bfloat16),
        ],
        compiler_params=pltpu.CompilerParams(vmem_limit_bytes=24 << 20),
        cost_estimate=pl.CostEstimate(
            flops=micro * tok * branch * (8 * width + 4 * tok),
            transcendentals=micro * tok * branch * 6,
            bytes_accessed=6 << 20,
        ),
        name="own",
    )(spot, lengths, valid, x, w_in)
    states = None
    for m in range(micro):
        operands = [spot, lengths, valid, arrived[m], x, w_in, w_out, gates, queries, mixed]
        specs = [SMEM] * 3 + [VMEM] * 7
        aliases = {}
        if states is not None:
            aliases = {len(operands): 0}
            operands.append(states)
            specs.append(ANY)
        states = pl.pallas_call(
            functools.partial(far_kernel, offset=m),
            out_shape=jax.ShapeDtypeStruct((1, micro, tok, width), jnp.bfloat16),
            grid=(1,),
            in_specs=specs,
            out_specs=pl.BlockSpec((1, 1, tok, width), lambda i, m=m: (0, m, 0, 0)),
            scratch_shapes=[
                pltpu.VMEM((tok, branch), jnp.bfloat16),
                pltpu.VMEM((tok, branch), jnp.bfloat16),
            ],
            input_output_aliases=aliases,
            compiler_params=pltpu.CompilerParams(vmem_limit_bytes=24 << 20),
            cost_estimate=pl.CostEstimate(
                flops=tok * branch * (6 * width + 4 * tok),
                transcendentals=tok * branch * 4,
                bytes_accessed=6 << 20,
            ),
            name="far",
        )(*operands)
    return states[0]


def shards(inputs, w_in, w_out, lengths, valid):
    micro, tok, width = inputs.shape
    sections = lax.axis_size("pipe")
    if sections == 1:
        return layer(inputs, w_in[0], w_out[0], lengths, valid, jnp.int32(0))[None]
    section = lax.axis_index("pipe")

    def tick(step, carry):
        incoming, states = carry
        slot = step - section
        active = (slot >= 0) & (slot < micro)
        index = jnp.clip(slot, 0, micro - 1)
        fresh = lax.dynamic_index_in_dim(inputs, index, 0, keepdims=False)
        x_rows = jnp.where(section == 0, fresh, incoming)
        result = layer(x_rows[None], w_in[0], w_out[0], lengths, valid, index)[0]
        updated = lax.dynamic_update_slice(
            states, result[None, None], (jnp.int32(0), index, jnp.int32(0), jnp.int32(0))
        )
        states = jnp.where(active, updated, states)
        return (shifted(result, "pipe", 1), states)

    start_states = jnp.zeros((1, micro, tok, width), jnp.bfloat16)
    start_rows = jnp.zeros((tok, width), jnp.bfloat16)
    _, states = lax.fori_loop(0, sections + micro - 1, tick, (start_rows, start_states))
    return states


def solution(mesh):
    in_specs = (P(None, "seq", None), P("pipe", None, None), P("pipe", None, None), P(), P())
    out_specs = P("pipe", None, "seq", None)
    return jax.shard_map(shards, mesh=mesh, in_specs=in_specs, out_specs=out_specs, check_vma=False)
```

time: 81.5 us -> 31.8 us (0.39)
  the two profiles are of different devices: /device:TPU:16 before, /device:TPU:0 now
where the time goes in v1:
time: 31.8 us; the launch traced here: 31.6 us
  Pallas kernels  21.6 us (68%)
  starting transfers between devices  6.93 us (22%)
  local copies, waits for them, and re-layouts  2.96 us (9%)
    pallas_call x2, Pallas kernels, layer(): pl.pallas_call(functools.partial(far_kernel, offset=m), out_shape=jax.Sha...  12.9 us
    pallas_call x1, Pallas kernels, layer(): pl.pallas_call(functools.partial(own_kernel, micro=micro), out_shape=(jax...  8.66 us
    ppermute x2, starting transfers between devices, shifted(): return lax.ppermute(x, axis, pairs)  6.93 us
    unnamed x10, local copies, waits for them, and re-layouts  1.6 us
    squeeze x1, local copies, waits for them, and re-layouts, layer(): arrived = [shifted(x[m], 'seq', 1) for m in range(micro)]  1.36 us
  transfers between devices with their start and end apart: 2, of which 0 were waited for; matrix products, arithmetic and copies ran while one was open for 0% of the time, Pallas kernels for 48%

profile of v1, /device:TPU:0, one launch (start us, length us, event | category | flops | bytes accessed | tf_op | source)
XLA Modules:
  0.0 31.6 jit_solution(13839929390866273289)
XLA Ops:
  0.0 0.0 copy-start
  0.0 0.0 copy-start.4
  0.0 0.0 copy-start.3
  0.0 1.4 %slice_bitcast_fusion = (bf16[512,512]{1,0:T(8,128)(2,1)S(1)}, bf16[512,512]{1,0:T(8,128)(2,1)S(1)}) fusion(bf16[2,512,512]{2,1,0:T(8,128)(2,1)} %x.5), kind=kLoop, calls=%fused_computation | loop fusion | bytes 2097152 | tf_op jit(solution)/shard_map/squeeze | solution.py:162
  1.4 2.4 %collective-permute-start.1 = (bf16[512,512]{1,0:T(8,128)(2,1)S(1)}, bf16[512,512]{1,0:T(8,128)(2,1)S(1)}, u32[]{:S(2)}, u32[]{:S(2)}) collective-permute-start(bf16[512,512]{1,0:T(8,128)(2,1)S(1)} %get-tuple-element.11), channel_id=1, source_target_pairs={{0,1},{1,2},{2,3},{3,4},{4,5},{5,6},{6,7},{7,8},{8,9},{9,10},{10,1... | collective-permute-start | bytes 1572872 | tf_op jit(solution)/shard_map/ppermute | solution.py:25
  3.8 4.5 %collective-permute-start = (bf16[512,512]{1,0:T(8,128)(2,1)S(1)}, bf16[512,512]{1,0:T(8,128)(2,1)S(1)}, u32[]{:S(2)}, u32[]{:S(2)}) collective-permute-start(bf16[512,512]{1,0:T(8,128)(2,1)S(1)} %get-tuple-element.12), channel_id=1, source_target_pairs={{0,1},{1,2},{2,3},{3,4},{4,5},{5,6},{6,7},{7,8},{8,9},{9,10},{10,1... | collective-permute-start | bytes 1572872 | tf_op jit(solution)/shard_map/ppermute | solution.py:25
  8.3 0.1 pad_add_fusion.spot
  8.4 0.0 copy-done
  8.4 0.0 copy-done.4
  8.4 0.0 copy-done.3
  8.4 0.0 copy-start.1
  8.4 1.6 %copy-done.1 = bf16[1,512,2048]{2,1,0:T(8,128)(2,1)S(1)} copy-done((bf16[1,512,2048]{2,1,0:T(8,128)(2,1)S(1)}, bf16[1,512,2048]{2,1,0:T(8,128)(2,1)}, u32[]{:S(2)}) %copy-start.1) | copy-done | bytes 2097176
  10.0 0.0 copy-start.2
  10.0 8.7 %own.1 = (bf16[2,512,512]{2,1,0:T(8,128)(2,1)S(1)}, bf16[2,512,512]{2,1,0:T(8,128)(2,1)S(1)}, f32[2,512,512]{2,1,0:T(8,128)S(1)}) custom-call(s32[2]{0:T(128)S(1)} %pad_add_fusion.spot, s32[2,8]{1,0:T(2,128)S(1)} %copy-done.3, s32[2,32]{1,0:T(2,128)S(1)} %copy-done.4, bf16[2,512,512]{2,1,0:T(8,128)(2,1)S(1)} %copy-done, bf16[512,2048]{1,0:T(8,128)(2,1)S(1)} %bitcast.7), custom_call_target="tpu_custom_call" | custom-call | flops 3221225472 | bytes 6291456 | tf_op jit(solution)/shard_map/own/pallas_call | solution.py:163
  18.7 0.0 collective-permute-done.1.before
  18.7 0.0 copy-done.2
  18.7 6.5 %far.2.rest_0_ = bf16[1,2,512,512]{3,2,1,0:T(8,128)(2,1)} custom-call(s32[2]{0:T(128)S(1)} %pad_add_fusion.spot, s32[2,8]{1,0:T(2,128)S(1)} %copy-done.3, s32[2,32]{1,0:T(2,128)S(1)} %copy-done.4, bf16[512,512]{1,0:T(8,128)(2,1)S(1)} %collective-permute-done.1.before, bf16[2,512,512]{2,1,0:T(8,128)(2,1)S(1)} %copy-done, bf16[512,2048]{1,0:T(8,128)(2,1)S(1)} %bitcast.8, ...), custom_call_target="tpu_custom_call" | custom-call | flops 1342177280 | bytes 6291456 | tf_op jit(solution)/shard_map/far/pallas_call | solution.py:193
  25.1 0.0 collective-permute-done.before
  25.1 6.5 %far.3 = bf16[1,2,512,512]{3,2,1,0:T(8,128)(2,1)} custom-call(s32[2]{0:T(128)S(1)} %pad_add_fusion.spot, s32[2,8]{1,0:T(2,128)S(1)} %copy-done.3, s32[2,32]{1,0:T(2,128)S(1)} %copy-done.4, bf16[512,512]{1,0:T(8,128)(2,1)S(1)} %collective-permute-done.before, bf16[2,512,512]{2,1,0:T(8,128)(2,1)S(1)} %copy-done, ...), custom_call_target="tpu_custom_call", output_to_operand_aliasing={{}: (10, {})} | custom-call | flops 1342177280 | bytes 6291456 | tf_op jit(solution)/shard_map/far/pallas_call | solution.py:193
Async XLA Ops:
  0.0 8.4 %copy-start = (bf16[2,512,512]{2,1,0:T(8,128)(2,1)S(1)}, bf16[2,512,512]{2,1,0:T(8,128)(2,1)}, u32[]{:S(2)}) copy-start(bf16[2,512,512]{2,1,0:T(8,128)(2,1)} %x.5) | copy-start | bytes 3145732
  0.0 8.4 %copy-start.4 = (s32[2,32]{1,0:T(2,128)S(1)}, s32[2,32]{1,0:T(2,128)}, u32[]{:S(2)}) copy-start(s32[2,32]{1,0:T(2,128)} %valid.5) | copy-start | bytes 772
  0.0 8.4 %copy-start.3 = (s32[2,8]{1,0:T(2,128)S(1)}, s32[2,8]{1,0:T(2,128)}, u32[]{:S(2)}) copy-start(s32[2,8]{1,0:T(2,128)} %lengths.5) | copy-start | bytes 196
  1.4 17.3 %collective-permute-start.1 = (bf16[512,512]{1,0:T(8,128)(2,1)S(1)}, bf16[512,512]{1,0:T(8,128)(2,1)S(1)}, u32[]{:S(2)}, u32[]{:S(2)}) collective-permute-start(bf16[512,512]{1,0:T(8,128)(2,1)S(1)} %get-tuple-element.11), channel_id=1, source_target_pairs={{0,1},{1,2},{2,3},{3,4},{4,5},{5,6},{6,7},{7,8},{8,9},{9,10},{10,1... | collective-permute-start | bytes 1572872 | tf_op jit(solution)/shard_map/ppermute | solution.py:25
  3.8 21.3 %collective-permute-start = (bf16[512,512]{1,0:T(8,128)(2,1)S(1)}, bf16[512,512]{1,0:T(8,128)(2,1)S(1)}, u32[]{:S(2)}, u32[]{:S(2)}) collective-permute-start(bf16[512,512]{1,0:T(8,128)(2,1)S(1)} %get-tuple-element.12), channel_id=1, source_target_pairs={{0,1},{1,2},{2,3},{3,4},{4,5},{5,6},{6,7},{7,8},{8,9},{9,10},{10,1... | collective-permute-start | bytes 1572872 | tf_op jit(solution)/shard_map/ppermute | solution.py:25
  8.4 1.6 %copy-start.1 = (bf16[1,512,2048]{2,1,0:T(8,128)(2,1)S(1)}, bf16[1,512,2048]{2,1,0:T(8,128)(2,1)}, u32[]{:S(2)}) copy-start(bf16[1,512,2048]{2,1,0:T(8,128)(2,1)} %param.6) | copy-start | bytes 6291460
  10.0 8.7 %copy-start.2 = (bf16[1,512,512]{2,1,0:T(8,128)(2,1)S(1)}, bf16[1,512,512]{2,1,0:T(8,128)(2,1)}, u32[]{:S(2)}) copy-start(bf16[1,512,512]{2,1,0:T(8,128)(2,1)} %param.7) | copy-start | bytes 1572868

commit v2 on v0

v2 whole, which is shorter than its diff:
```python
import functools
import math

import jax
import jax.numpy as jnp
from jax import lax
from jax.experimental import pallas as pl
from jax.experimental.pallas import tpu as pltpu
from jax.sharding import PartitionSpec as P

HEAD_DIM = 128
WINDOW = 512
BLOCK = 256
LATE = (3, 4)

norm_eps = 1e-05
out_eps = 0.001

FAR = 1 << 30


def shifted(x, axis, by):
    size = lax.axis_size(axis)
    pairs = [(i, i + by) for i in range(size) if 0 <= i + by < size]
    return lax.ppermute(x, axis, pairs)


def normalise(values, epsilon, factor=1.0):
    mean = jnp.mean(values, axis=-1, keepdims=True)
    centred = values - mean
    spread = jnp.mean(centred * centred, axis=-1, keepdims=True)
    return centred * (factor * lax.rsqrt(spread + epsilon))


def half_silu(half):
    return half + half * jnp.tanh(half)


def dot(a, b):
    return jnp.dot(a, b, preferred_element_type=jnp.float32)


def dot_rows(a, b):
    return lax.dot_general(a, b, (((1,), (1,)), ((), ())), preferred_element_type=jnp.float32)


def lanes(head):
    return slice(head * HEAD_DIM, (head + 1) * HEAD_DIM)


def wide(columns, width):
    return jnp.concatenate([columns] * (width // columns.shape[1]), 1)


def places(top, bottom, left, right):
    shape = (bottom - top, right - left)
    row = top + lax.broadcasted_iota(jnp.int32, shape, 0)
    col = left + lax.broadcasted_iota(jnp.int32, shape, 1)
    return row, col


def local_blocks(low, high):
    edges = [low, *[e for e in range(0, high, BLOCK) if e > low], high]
    return list(zip(edges[:-1], edges[1:]))


def rows_of(first, second, micro, tok, m, top, bottom):
    late = second.shape[0]
    if m < micro - 1:
        return first[m * tok + top : m * tok + bottom, :]
    if top >= late:
        return first[m * tok + top - late : m * tok + bottom - late, :]
    if bottom <= late:
        return second[top:bottom, :]
    return jnp.concatenate([second[top:late, :], first[m * tok : m * tok + bottom - late, :]], 0)


def cut_kernel(x, first, second, sems):
    micro, tok, _ = x.shape
    late = second.shape[0]
    last = micro - 1
    copies = [
        (x.at[m], first.at[pl.ds(m * tok, tok)]) for m in range(last)
    ] + [
        (x.at[last, pl.ds(late, tok - late)], first.at[pl.ds(last * tok, tok - late)]),
        (x.at[last, pl.ds(0, late)], second),
    ]
    copies = [pltpu.make_async_copy(a, b, sems.at[i]) for i, (a, b) in enumerate(copies)]
    for copy in copies:
        copy.start()
    for copy in copies:
        copy.wait()


def own_kernel(
    slot, first, second, w_in, lengths, valid,
    gates, queries, mixed, w_kv, floors, counts,
    w_q, w_u, normed, keys, values, spans, alive, sems,
    *, micro, tok,
):
    branch = w_q.shape[1]
    heads = branch // HEAD_DIM
    scale = 0.5 / math.sqrt(HEAD_DIM)
    block = lax.axis_index("seq")
    parts = {
        1: (w_kv.at[:, pl.ds(0, branch)], values),
        3: (w_kv.at[:, pl.ds(branch, branch)], keys),
        2: (w_q, queries),
        0: (w_u, gates),
    }
    small = [
        pltpu.make_async_copy(lengths, spans, sems.at[4]),
        pltpu.make_async_copy(valid, alive, sems.at[5]),
    ]
    loads = {
        part: pltpu.make_async_copy(w_in.at[:, pl.ds(part * branch, branch)], there, sems.at[part])
        for part, (there, _) in parts.items()
    }
    for copy in [*loads.values(), *small]:
        copy.start()
    for m in range(micro):
        for top in range(0, tok, 128):
            rows = rows_of(first, second, micro, tok, m, top, top + 128).astype(jnp.float32)
            normed[m * tok + top : m * tok + top + 128, :] = normalise(rows, norm_eps, 0.5).astype(
                jnp.bfloat16
            )
    for part, (weight, kept) in parts.items():
        loads[part].wait()
        for m in range(micro):
            out = half_silu(dot(normed[m * tok : (m + 1) * tok, :], weight[...]))
            kept[m] = (out * scale if part == 2 else out).astype(jnp.bfloat16)
    for copy in small:
        copy.wait()
    for m in range(micro):
        row = lax.broadcasted_iota(jnp.int32, (tok, 128), 0)
        place = block * tok + row
        bound = jnp.int32(0)
        start = jnp.zeros((tok, 128), jnp.int32)
        for k in range(spans.shape[1]):
            bound = bound + spans[slot + m, k]
            start = jnp.where(place >= bound, bound, start)
        floors[m] = jnp.where(row < alive[slot + m, block], start - block * tok, FAR)
        counts[m] = jnp.full((8, 128), alive[slot + m, jnp.maximum(block - 1, 0)], jnp.int32)
    pending = []

    def finish(m, head, pieces):
        total = {}
        for (left, right), weights in pieces:
            product = dot(weights, values[m, left:right, lanes(head)])
            for top in range(left, tok, BLOCK):
                piece = product[top - left : top - left + BLOCK]
                total[top] = total[top] + piece if top in total else piece
        mixed[m, :, lanes(head)] = jnp.concatenate([total[t] for t in sorted(total)], 0)

    for m in range(micro):
        masks = {}
        for left, right in local_blocks(0, tok):
            row, col = places(left, tok, left, right)
            masks[left] = (col <= row) & (col >= wide(floors[m, left:tok], right - left))
        for head in range(heads):
            pieces = []
            for left, right in local_blocks(0, tok):
                half = dot_rows(queries[m, left:tok, lanes(head)], keys[m, left:right, lanes(head)])
                weights = jnp.where(masks[left], half_silu(half), 0.0).astype(jnp.bfloat16)
                pieces.append(((left, right), weights))
            pending.append((m, head, pieces))
            if len(pending) > 1:
                finish(*pending.pop(0))
    finish(*pending.pop(0))


def far_rows(before, w_kv, keys, values):
    branch = keys.shape[1]
    rows = before.shape[0]
    for top in range(0, rows, BLOCK):
        bottom = min(top + BLOCK, rows)
        normed = normalise(before[top:bottom, :].astype(jnp.float32), norm_eps, 0.5)
        normed = normed.astype(jnp.bfloat16)
        values[top:bottom, :] = half_silu(dot(normed, w_kv[:, :branch])).astype(jnp.bfloat16)
        keys[top:bottom, :] = half_silu(dot(normed, w_kv[:, branch:])).astype(jnp.bfloat16)


def far_sums(low, high, offset, queries, mixed, floors, counts, keys, values, m, tok):
    blocks = local_blocks(low, high)[::-1]
    edges = sorted({0, *[e for b in blocks for e in b if e > 0]})
    masks = {}
    for left, right in blocks:
        row, col = places(0, right, left, right)
        reach = wide(jnp.concatenate([counts[m]] * (right // 8), 0), right - left)
        earliest = wide(floors[m, 0:right], right - left) + tok
        masks[left] = (col > row) & (col >= earliest) & (col < reach)
    sums = []
    pending = []

    def finish(head, pieces):
        total = {top: mixed[m, top:bottom, lanes(head)] for top, bottom in zip(edges, edges[1:])}
        for (left, right), weights in pieces:
            product = dot(weights, values[offset + left : offset + right, lanes(head)])
            for top, bottom in zip(edges, edges[1:]):
                if bottom <= right:
                    total[top] = total[top] + product[top:bottom]
        sums.append(jnp.concatenate([total[t] for t in sorted(total)], 0))

    for head in range(queries.shape[2] // HEAD_DIM):
        pieces = []
        for left, right in blocks:
            half = dot_rows(
                queries[m, 0:right, lanes(head)],
                keys[offset + left : offset + right, lanes(head)],
            )
            weights = jnp.where(masks[left], half_silu(half), 0.0).astype(jnp.bfloat16)
            pieces.append(((left, right), weights))
        pending.append((head, pieces))
        if len(pending) > 1:
            finish(*pending.pop(0))
    finish(*pending.pop(0))
    return sums


def close(sums, top, bottom, x_rows, w_out, gates, m, done, out, sems, number):
    copies = []
    for low in range(top, bottom, BLOCK):
        high = min(low + BLOCK, bottom)
        attended = jnp.concatenate([s[low:high] for s in sums], 1)
        attended = normalise(attended, out_eps * WINDOW)
        gated = (attended * gates[m, low:high, :].astype(jnp.float32)).astype(jnp.bfloat16)
        result = x_rows(m, low, high).astype(jnp.float32) + dot(gated, w_out[...])
        done[m, low:high, :] = result.astype(jnp.bfloat16)
        copies.append(
            pltpu.make_async_copy(
                done.at[m, pl.ds(low, high - low)],
                out.at[0, m, pl.ds(low, high - low)],
                sems.at[number + len(copies)],
            )
        )
        copies[-1].start()
    return copies


def far_first_kernel(
    before, first, second, w_kv, w_out, gates, queries, mixed, floors, counts,
    out, rest, keys, values, done, sems, *, micro, tok,
):
    late = second.shape[0]
    last = micro - 1
    x_rows = functools.partial(rows_of, first, second, micro, tok)
    far_rows(before, w_kv, keys, values)
    copies = []
    for m in range(last):
        sums = far_sums(0, tok, m * tok, queries, mixed, floors, counts, keys, values, m, tok)
        copies += close(sums, 0, tok, x_rows, w_out, gates, m, done, out, sems, len(copies))
    sums = far_sums(
        late, tok, last * tok - late, queries, mixed, floors, counts, keys, values, last, tok
    )
    for head, total in enumerate(sums):
        rest[0, :, lanes(head)] = total[:late]
    copies += close(sums, late, tok, x_rows, w_out, gates, last, done, out, sems, len(copies))
    for copy in copies:
        copy.wait()


def far_second_kernel(
    before, second, w_kv, w_out, gates, queries, rest, floors, counts, _,
    out, keys, values, done, sems, *, tok,
):
    late = second.shape[0]
    last = gates.shape[0] - 1
    far_rows(before, w_kv, keys, values)

    class Last:
        def __getitem__(self, index):
            return rest[(0, *index[1:])]

    sums = far_sums(0, late, 0, queries, Last(), floors, counts, keys, values, last, tok)
    for copy in close(
        sums, 0, late, lambda m, top, bottom: second[top:bottom, :],
        w_out, gates, last, done, out, sems, 0,
    ):
        copy.wait()


VMEM = pl.BlockSpec(memory_space=pltpu.VMEM)
SMEM = pl.BlockSpec(memory_space=pltpu.SMEM)
HBM = pl.BlockSpec(memory_space=pltpu.HBM)


def layer(x, w_in, w_out, lengths, valid, slot):
    micro, tok, width = x.shape
    branch = w_out.shape[0]
    late = tok * LATE[0] // LATE[1]
    early = micro * tok - late
    bf16, f32, i32 = jnp.bfloat16, jnp.float32, jnp.int32
    shape = jax.ShapeDtypeStruct
    params = pltpu.CompilerParams(vmem_limit_bytes=24 << 20)

    def cost(rows, flops, tanhs):
        return pl.CostEstimate(
            flops=rows * flops, transcendentals=rows * tanhs, bytes_accessed=4 << 20
        )

    first, second = pl.pallas_call(
        cut_kernel,
        out_shape=(shape((early, width), bf16), shape((late, width), bf16)),
        in_specs=[HBM],
        out_specs=(VMEM, VMEM),
        scratch_shapes=[pltpu.SemaphoreType.DMA((micro + 1,))],
        compiler_params=params,
        name="cut",
    )(x)
    first_come = shifted(first, "seq", 1)
    second_come = shifted(second, "seq", 1)

    gates, queries, mixed, w_kv, floors, counts = pl.pallas_call(
        functools.partial(own_kernel, slot, micro=micro, tok=tok)
        if isinstance(slot, int)
        else functools.partial(own_kernel_at, micro=micro, tok=tok),
        out_shape=(
            shape((micro, tok, branch), bf16),
            shape((micro, tok, branch), bf16),
            shape((micro, tok, branch), f32),
            shape((width, 2 * branch), bf16),
            shape((micro, tok, 128), i32),
            shape((micro, 8, 128), i32),
        ),
        in_specs=([] if isinstance(slot, int) else [SMEM]) + [VMEM, VMEM, HBM, HBM, HBM],
        out_specs=(VMEM,) * 6,
        scratch_shapes=[
            pltpu.VMEM((width, branch), bf16),
            pltpu.VMEM((width, branch), bf16),
            pltpu.VMEM((micro * tok, width), bf16),
            pltpu.VMEM((micro, tok, branch), bf16),
            pltpu.VMEM((micro, tok, branch), bf16),
            pltpu.SMEM(lengths.shape, i32),
            pltpu.SMEM(valid.shape, i32),
            pltpu.SemaphoreType.DMA((6,)),
        ],
        compiler_params=params,
        cost_estimate=cost(micro * tok, branch * (8 * width + 4 * tok), branch * 6),
        name="own",
    )(*([] if isinstance(slot, int) else [slot[None]]), first, second, w_in, lengths, valid)
    states, rest = pl.pallas_call(
        functools.partial(far_first_kernel, micro=micro, tok=tok),
        out_shape=(shape((1, micro, tok, width), bf16), shape((1, late, branch), f32)),
        in_specs=[VMEM] * 10,
        out_specs=(HBM, VMEM),
        scratch_shapes=[
            pltpu.VMEM((early, branch), bf16),
            pltpu.VMEM((early, branch), bf16),
            pltpu.VMEM((micro, tok, width), bf16),
            pltpu.SemaphoreType.DMA((micro * (tok // BLOCK + 1),)),
        ],
        compiler_params=params,
        cost_estimate=cost(early, branch * (6 * width + 4 * tok), branch * 4),
        name="far_first",
    )(first_come, first, second, w_kv, w_out, gates, queries, mixed, floors, counts)
    return pl.pallas_call(
        functools.partial(far_second_kernel, tok=tok),
        out_shape=shape((1, micro, tok, width), bf16),
        in_specs=[VMEM] * 9 + [HBM],
        out_specs=HBM,
        scratch_shapes=[
            pltpu.VMEM((late, branch), bf16),
            pltpu.VMEM((late, branch), bf16),
            pltpu.VMEM((micro, tok, width), bf16),
            pltpu.SemaphoreType.DMA((late // BLOCK + 1,)),
        ],
        input_output_aliases={9: 0},
        compiler_params=params,
        cost_estimate=cost(late, branch * (6 * width + 4 * tok), branch * 4),
        name="far_second",
    )(second_come, second, w_kv, w_out, gates, queries, rest, floors, counts, states)[0]


def own_kernel_at(slot, *refs, micro, tok):
    own_kernel(slot[0], *refs, micro=micro, tok=tok)


def shards(inputs, w_in, w_out, lengths, valid):
    micro, tok, width = inputs.shape
    sections = lax.axis_size("pipe")
    if sections == 1:
        return layer(inputs, w_in[0], w_out[0], lengths, valid, 0)[None]
    section = lax.axis_index("pipe")

    def tick(step, carry):
        incoming, states = carry
        slot = step - section
        active = (slot >= 0) & (slot < micro)
        index = jnp.clip(slot, 0, micro - 1)
        fresh = lax.dynamic_index_in_dim(inputs, index, 0, keepdims=False)
        x_rows = jnp.where(section == 0, fresh, incoming)
        result = layer(x_rows[None], w_in[0], w_out[0], lengths, valid, index)[0]
        updated = lax.dynamic_update_slice(
            states, result[None, None], (jnp.int32(0), index, jnp.int32(0), jnp.int32(0))
        )
        states = jnp.where(active, updated, states)
        return (shifted(result, "pipe", 1), states)

    start_states = jnp.zeros((1, micro, tok, width), jnp.bfloat16)
    start_rows = jnp.zeros((tok, width), jnp.bfloat16)
    _, states = lax.fori_loop(0, sections + micro - 1, tick, (start_rows, start_states))
    return states


def solution(mesh):
    in_specs = (P(None, "seq", None), P("pipe", None, None), P("pipe", None, None), P(), P())
    out_specs = P("pipe", None, "seq", None)
    return jax.shard_map(shards, mesh=mesh, in_specs=in_specs, out_specs=out_specs, check_vma=False)
```

time: 81.5 us -> 25.1 us (0.31)
  the two profiles are of different devices: /device:TPU:16 before, /device:TPU:0 now
where the time goes in v2:
time: 25.1 us; the launch traced here: 24.9 us
  Pallas kernels  13.7 us (55%)
  starting transfers between devices  6.92 us (28%)
  local copies, waits for them, and re-layouts  4.17 us (17%)
    ppermute x2, starting transfers between devices, shifted(): return lax.ppermute(x, axis, pairs)  6.92 us
    pallas_call x1, Pallas kernels, layer(): pl.pallas_call(functools.partial(own_kernel, slot, micro=micro, tok=tok)...  6.29 us
    pallas_call x1, Pallas kernels, layer(): pl.pallas_call(functools.partial(far_first_kernel, micro=micro, tok=tok),...  4.19 us
    unnamed x10, local copies, waits for them, and re-layouts  4.17 us
    pallas_call x1, Pallas kernels, layer(): pl.pallas_call(functools.partial(far_second_kernel, tok=tok), out_shape=s...  2.79 us
  transfers between devices with their start and end apart: 2, of which 0 were waited for; matrix products, arithmetic and copies ran while one was open for 0% of the time, Pallas kernels for 42%

profile of v2, /device:TPU:0, one launch (start us, length us, event | category | flops | bytes accessed | tf_op | source)
XLA Modules:
  0.0 24.9 jit_solution(12680982909908327708)
XLA Ops:
  0.0 0.0 copy-start.1
  0.0 1.2 %copy-done.1 = bf16[2,512,512]{2,1,0:T(8,128)(2,1)S(1)} copy-done((bf16[2,512,512]{2,1,0:T(8,128)(2,1)S(1)}, bf16[2,512,512]{2,1,0:T(8,128)(2,1)}, u32[]{:S(2)}) %copy-start.1) | copy-done | bytes 1048600
  1.2 0.4 %cut.1 = (bf16[640,512]{1,0:T(8,128)(2,1)S(1)}, bf16[384,512]{1,0:T(8,128)(2,1)S(1)}) custom-call(bf16[2,512,512]{2,1,0:T(8,128)(2,1)S(1)} %copy-done.1), custom_call_target="tpu_custom_call" | custom-call | tf_op jit(solution)/shard_map/cut/pallas_call | solution.py:301
  1.7 2.4 %collective-permute-start.1 = (bf16[640,512]{1,0:T(8,128)(2,1)S(1)}, bf16[640,512]{1,0:T(8,128)(2,1)S(1)}, u32[]{:S(2)}, u32[]{:S(2)}) collective-permute-start(bf16[640,512]{1,0:T(8,128)(2,1)S(1)} %get-tuple-element.16.first), channel_id=1, source_target_pairs={{0,1},{1,2},{2,3},{3,4},{4,5},{5,6},{6,7},{7,8},{8,9},{9,10},{10,1... | collective-permute-start | bytes 1966088 | tf_op jit(solution)/shard_map/ppermute | solution.py:25
  4.1 4.5 %collective-permute-start = (bf16[384,512]{1,0:T(8,128)(2,1)S(1)}, bf16[384,512]{1,0:T(8,128)(2,1)S(1)}, u32[]{:S(2)}, u32[]{:S(2)}) collective-permute-start(bf16[384,512]{1,0:T(8,128)(2,1)S(1)} %get-tuple-element.15.second), channel_id=1, source_target_pairs={{0,1},{1,2},{2,3},{3,4},{4,5},{5,6},{6,7},{7,8},{8,9},{9,10},{10,1... | collective-permute-start | bytes 1179656 | tf_op jit(solution)/shard_map/ppermute | solution.py:25
  8.6 0.0 copy-start.2
  8.6 1.6 %copy-done.2 = bf16[1,512,2048]{2,1,0:T(8,128)(2,1)S(1)} copy-done((bf16[1,512,2048]{2,1,0:T(8,128)(2,1)S(1)}, bf16[1,512,2048]{2,1,0:T(8,128)(2,1)}, u32[]{:S(2)}) %copy-start.2) | copy-done | bytes 2097176
  10.2 0.0 copy-start.3
  10.2 0.7 %copy-done.3 = s32[2,8]{1,0:T(2,128)S(1)} copy-done((s32[2,8]{1,0:T(2,128)S(1)}, s32[2,8]{1,0:T(2,128)}, u32[]{:S(2)}) %copy-start.3) | copy-done | bytes 88
  10.9 0.0 copy-start.4
  10.9 0.7 %copy-done.4 = s32[2,32]{1,0:T(2,128)S(1)} copy-done((s32[2,32]{1,0:T(2,128)S(1)}, s32[2,32]{1,0:T(2,128)}, u32[]{:S(2)}) %copy-start.4) | copy-done | bytes 280
  11.5 0.0 copy-start
  11.5 6.3 %own.1 = (bf16[2,512,512]{2,1,0:T(8,128)(2,1)S(1)}, bf16[2,512,512]{2,1,0:T(8,128)(2,1)S(1)}, f32[2,512,512]{2,1,0:T(8,128)S(1)}, bf16[512,1024]{1,0:T(8,128)(2,...) custom-call(bf16[640,512]{1,0:T(8,128)(2,1)S(1)} %get-tuple-element.16.first, ...), custom_call_target="tpu_custom_call" | custom-call | flops 3221225472 | bytes 4194304 | tf_op jit(solution)/shard_map/own/pallas_call | solution.py:313
  17.8 0.0 collective-permute-done.1.before
  17.9 0.0 copy-done
  17.9 4.2 %far_first.1 = (bf16[1,2,512,512]{3,2,1,0:T(8,128)(2,1)}, f32[1,384,512]{2,1,0:T(8,128)S(1)}) custom-call(bf16[640,512]{1,0:T(8,128)(2,1)S(1)} %collective-permute-done.1.before, bf16[640,512]{1,0:T(8,128)(2,1)S(1)} %get-tuple-element.16.first, bf16[384,512]{1,0:T(8,128)(2,1)S(1)} %get-tuple-element.15.second, bf16[512,1024]{1,0:T(8,128)(2,1)S(1)} %get-tuple-element.17.w_kv, ...), custom_call_target="tpu_custom_call" | custom-call | flops 1677721600 | bytes 4194304 | tf_op jit(solution)/shard_map/far_first/pallas_call | solution.py:341
  22.1 0.0 collective-permute-done.before
  22.1 2.8 %far_second.1 = bf16[1,2,512,512]{3,2,1,0:T(8,128)(2,1)} custom-call(bf16[384,512]{1,0:T(8,128)(2,1)S(1)} %collective-permute-done.before, bf16[384,512]{1,0:T(8,128)(2,1)S(1)} %get-tuple-element.15.second, bf16[512,1024]{1,0:T(8,128)(2,1)S(1)} %get-tuple-element.17.w_kv, bf16[512,512]{1,0:T(8,128)(2,1)S(1)} %bitcast.3, ...), custom_call_target="tpu_custom_call", output_to_operand_aliasing={{}: (9, {})} | custom-call | flops 1006632960 | bytes 4194304 | tf_op jit(solution)/shard_map/far_second/pallas_call | solution.py:356
Async XLA Ops:
  0.0 1.2 %copy-start.1 = (bf16[2,512,512]{2,1,0:T(8,128)(2,1)S(1)}, bf16[2,512,512]{2,1,0:T(8,128)(2,1)}, u32[]{:S(2)}) copy-start(bf16[2,512,512]{2,1,0:T(8,128)(2,1)} %x.1) | copy-start | bytes 3145732
  1.7 16.2 %collective-permute-start.1 = (bf16[640,512]{1,0:T(8,128)(2,1)S(1)}, bf16[640,512]{1,0:T(8,128)(2,1)S(1)}, u32[]{:S(2)}, u32[]{:S(2)}) collective-permute-start(bf16[640,512]{1,0:T(8,128)(2,1)S(1)} %get-tuple-element.16.first), channel_id=1, source_target_pairs={{0,1},{1,2},{2,3},{3,4},{4,5},{5,6},{6,7},{7,8},{8,9},{9,10},{10,1... | collective-permute-start | bytes 1966088 | tf_op jit(solution)/shard_map/ppermute | solution.py:25
  4.1 18.0 %collective-permute-start = (bf16[384,512]{1,0:T(8,128)(2,1)S(1)}, bf16[384,512]{1,0:T(8,128)(2,1)S(1)}, u32[]{:S(2)}, u32[]{:S(2)}) collective-permute-start(bf16[384,512]{1,0:T(8,128)(2,1)S(1)} %get-tuple-element.15.second), channel_id=1, source_target_pairs={{0,1},{1,2},{2,3},{3,4},{4,5},{5,6},{6,7},{7,8},{8,9},{9,10},{10,1... | collective-permute-start | bytes 1179656 | tf_op jit(solution)/shard_map/ppermute | solution.py:25
  8.6 1.6 %copy-start.2 = (bf16[1,512,2048]{2,1,0:T(8,128)(2,1)S(1)}, bf16[1,512,2048]{2,1,0:T(8,128)(2,1)}, u32[]{:S(2)}) copy-start(bf16[1,512,2048]{2,1,0:T(8,128)(2,1)} %param.6) | copy-start | bytes 6291460
  10.2 0.7 %copy-start.3 = (s32[2,8]{1,0:T(2,128)S(1)}, s32[2,8]{1,0:T(2,128)}, u32[]{:S(2)}) copy-start(s32[2,8]{1,0:T(2,128)} %lengths.1) | copy-start | bytes 196
  10.9 0.7 %copy-start.4 = (s32[2,32]{1,0:T(2,128)S(1)}, s32[2,32]{1,0:T(2,128)}, u32[]{:S(2)}) copy-start(s32[2,32]{1,0:T(2,128)} %valid.1) | copy-start | bytes 772
  11.5 6.3 %copy-start = (bf16[1,512,512]{2,1,0:T(8,128)(2,1)S(1)}, bf16[1,512,512]{2,1,0:T(8,128)(2,1)}, u32[]{:S(2)}) copy-start(bf16[1,512,512]{2,1,0:T(8,128)(2,1)} %param.7) | copy-start | bytes 1572868

commit v3 on v2

--- a/solution.py
+++ b/solution.py
@@ -284,6 +284,10 @@
 HBM = pl.BlockSpec(memory_space=pltpu.HBM)
 
 
+def kept_in_hbm(x):
+    return pltpu.with_memory_space_constraint(x, pltpu.HBM)
+
+
 def layer(x, w_in, w_out, lengths, valid, slot):
     micro, tok, width = x.shape
     branch = w_out.shape[0]
@@ -306,7 +310,7 @@
         scratch_shapes=[pltpu.SemaphoreType.DMA((micro + 1,))],
         compiler_params=params,
         name="cut",
-    )(x)
+    )(kept_in_hbm(x))
     first_come = shifted(first, "seq", 1)
     second_come = shifted(second, "seq", 1)
 
@@ -337,7 +341,7 @@
         compiler_params=params,
         cost_estimate=cost(micro * tok, branch * (8 * width + 4 * tok), branch * 6),
         name="own",
-    )(*([] if isinstance(slot, int) else [slot[None]]), first, second, w_in, lengths, valid)
+    )(*([] if isinstance(slot, int) else [slot[None]]), first, second, *map(kept_in_hbm, (w_in, lengths, valid)))
     states, rest = pl.pallas_call(
         functools.partial(far_first_kernel, micro=micro, tok=tok),
         out_shape=(shape((1, micro, tok, width), bf16), shape((1, late, branch), f32)),

time: 25.1 us -> 22.1 us (0.88)
  local copies, waits for them, and re-layouts: 4.17 us -> 0.01 us
  Pallas kernels: 13.7 us -> 14.9 us
    unnamed x10 -> x2, local copies, waits for them, and re-layouts: 4.17 us -> 0.01 us
    pallas_call x1, Pallas kernels: 0.42 us -> 1.22 us  [layer(): pl.pallas_call(cut_kernel, out_shape=(shape((early, width), bf16), shape(...]
    pallas_call x1, Pallas kernels: 6.29 us -> 6.76 us  [layer(): pl.pallas_call(functools.partial(own_kernel, slot, micro=micro, tok=tok)...]
  transfers between devices with their start and end apart: 2 -> 2, of which waited for: 0 -> 0; matrix products, arithmetic and copies ran while one was open for 0% -> 0% of each run, Pallas kernels for 42% -> 50%
where the time goes in v3:
time: 22.1 us; the launch traced here: 21.9 us
  Pallas kernels  14.9 us (67%)
  starting transfers between devices  6.92 us (31%)
    ppermute x2, starting transfers between devices, shifted(): return lax.ppermute(x, axis, pairs)  6.92 us
    pallas_call x1, Pallas kernels, layer(): pl.pallas_call(functools.partial(own_kernel, slot, micro=micro, tok=tok)...  6.76 us
    pallas_call x1, Pallas kernels, layer(): pl.pallas_call(functools.partial(far_first_kernel, micro=micro, tok=tok),...  4.16 us
    pallas_call x1, Pallas kernels, layer(): pl.pallas_call(functools.partial(far_second_kernel, tok=tok), out_shape=s...  2.78 us
    pallas_call x1, Pallas kernels, layer(): pl.pallas_call(cut_kernel, out_shape=(shape((early, width), bf16), shape(...  1.22 us
  transfers between devices with their start and end apart: 2, of which 0 were waited for; matrix products, arithmetic and copies ran while one was open for 0% of the time, Pallas kernels for 50%

profile of v3, /device:TPU:0, one launch (start us, length us, event | category | flops | bytes accessed | tf_op | source)
XLA Modules:
  0.0 21.9 jit_solution(11219901599367657918)
XLA Ops:
  0.0 1.2 %cut.1 = (bf16[640,512]{1,0:T(8,128)(2,1)S(1)}, bf16[384,512]{1,0:T(8,128)(2,1)S(1)}) custom-call(bf16[2,512,512]{2,1,0:T(8,128)(2,1)} %x.1), custom_call_target="tpu_custom_call" | custom-call | tf_op jit(solution)/shard_map/cut/pallas_call | solution.py:305
  1.2 2.4 %collective-permute-start.1 = (bf16[640,512]{1,0:T(8,128)(2,1)S(1)}, bf16[640,512]{1,0:T(8,128)(2,1)S(1)}, u32[]{:S(2)}, u32[]{:S(2)}) collective-permute-start(bf16[640,512]{1,0:T(8,128)(2,1)S(1)} %get-tuple-element.16.first), channel_id=1, source_target_pairs={{0,1},{1,2},{2,3},{3,4},{4,5},{5,6},{6,7},{7,8},{8,9},{9,10},{10,1... | collective-permute-start | bytes 1966088 | tf_op jit(solution)/shard_map/ppermute | solution.py:25
  3.7 4.5 %collective-permute-start = (bf16[384,512]{1,0:T(8,128)(2,1)S(1)}, bf16[384,512]{1,0:T(8,128)(2,1)S(1)}, u32[]{:S(2)}, u32[]{:S(2)}) collective-permute-start(bf16[384,512]{1,0:T(8,128)(2,1)S(1)} %get-tuple-element.15.second), channel_id=1, source_target_pairs={{0,1},{1,2},{2,3},{3,4},{4,5},{5,6},{6,7},{7,8},{8,9},{9,10},{10,1... | collective-permute-start | bytes 1179656 | tf_op jit(solution)/shard_map/ppermute | solution.py:25
  8.2 0.0 copy-start
  8.2 6.8 %own.1 = (bf16[2,512,512]{2,1,0:T(8,128)(2,1)S(1)}, bf16[2,512,512]{2,1,0:T(8,128)(2,1)S(1)}, f32[2,512,512]{2,1,0:T(8,128)S(1)}, bf16[512,1024]{1,0:T(8,128)(2,...) custom-call(bf16[640,512]{1,0:T(8,128)(2,1)S(1)} %get-tuple-element.16.first, ...), custom_call_target="tpu_custom_call" | custom-call | flops 3221225472 | bytes 4194304 | tf_op jit(solution)/shard_map/own/pallas_call | solution.py:317
  14.9 0.0 collective-permute-done.1.before
  14.9 0.0 copy-done
  15.0 4.2 %far_first.1 = (bf16[1,2,512,512]{3,2,1,0:T(8,128)(2,1)}, f32[1,384,512]{2,1,0:T(8,128)S(1)}) custom-call(bf16[640,512]{1,0:T(8,128)(2,1)S(1)} %collective-permute-done.1.before, bf16[640,512]{1,0:T(8,128)(2,1)S(1)} %get-tuple-element.16.first, bf16[384,512]{1,0:T(8,128)(2,1)S(1)} %get-tuple-element.15.second, bf16[512,1024]{1,0:T(8,128)(2,1)S(1)} %get-tuple-element.17.w_kv, ...), custom_call_target="tpu_custom_call" | custom-call | flops 1677721600 | bytes 4194304 | tf_op jit(solution)/shard_map/far_first/pallas_call | solution.py:345
  19.1 0.0 collective-permute-done.before
  19.1 2.8 %far_second.1 = bf16[1,2,512,512]{3,2,1,0:T(8,128)(2,1)} custom-call(bf16[384,512]{1,0:T(8,128)(2,1)S(1)} %collective-permute-done.before, bf16[384,512]{1,0:T(8,128)(2,1)S(1)} %get-tuple-element.15.second, bf16[512,1024]{1,0:T(8,128)(2,1)S(1)} %get-tuple-element.17.w_kv, bf16[512,512]{1,0:T(8,128)(2,1)S(1)} %bitcast.3, ...), custom_call_target="tpu_custom_call", output_to_operand_aliasing={{}: (9, {})} | custom-call | flops 1006632960 | bytes 4194304 | tf_op jit(solution)/shard_map/far_second/pallas_call | solution.py:360
Async XLA Ops:
  1.2 13.7 %collective-permute-start.1 = (bf16[640,512]{1,0:T(8,128)(2,1)S(1)}, bf16[640,512]{1,0:T(8,128)(2,1)S(1)}, u32[]{:S(2)}, u32[]{:S(2)}) collective-permute-start(bf16[640,512]{1,0:T(8,128)(2,1)S(1)} %get-tuple-element.16.first), channel_id=1, source_target_pairs={{0,1},{1,2},{2,3},{3,4},{4,5},{5,6},{6,7},{7,8},{8,9},{9,10},{10,1... | collective-permute-start | bytes 1966088 | tf_op jit(solution)/shard_map/ppermute | solution.py:25
  3.7 15.5 %collective-permute-start = (bf16[384,512]{1,0:T(8,128)(2,1)S(1)}, bf16[384,512]{1,0:T(8,128)(2,1)S(1)}, u32[]{:S(2)}, u32[]{:S(2)}) collective-permute-start(bf16[384,512]{1,0:T(8,128)(2,1)S(1)} %get-tuple-element.15.second), channel_id=1, source_target_pairs={{0,1},{1,2},{2,3},{3,4},{4,5},{5,6},{6,7},{7,8},{8,9},{9,10},{10,1... | collective-permute-start | bytes 1179656 | tf_op jit(solution)/shard_map/ppermute | solution.py:25
  8.2 6.8 %copy-start = (bf16[1,512,512]{2,1,0:T(8,128)(2,1)S(1)}, bf16[1,512,512]{2,1,0:T(8,128)(2,1)}, u32[]{:S(2)}) copy-start(bf16[1,512,512]{2,1,0:T(8,128)(2,1)} %param.7) | copy-start | bytes 1572868

commit v4 on v3

v4 whole, which is shorter than its diff:
```python
import functools
import math

import jax
import jax.numpy as jnp
from jax import lax
from jax.experimental import pallas as pl
from jax.experimental.pallas import tpu as pltpu
from jax.sharding import PartitionSpec as P

HEAD_DIM = 128
WINDOW = 512
BLOCK = 256
LATE_OTHER = 4
LATE_LAST = 2

norm_eps = 1e-05
out_eps = 0.001

FAR = 1 << 30


def shifted(x, axis, by):
    size = lax.axis_size(axis)
    pairs = [(i, i + by) for i in range(size) if 0 <= i + by < size]
    return lax.ppermute(x, axis, pairs)


def normalise(values, epsilon, factor=1.0):
    mean = jnp.mean(values, axis=-1, keepdims=True)
    centred = values - mean
    spread = jnp.mean(centred * centred, axis=-1, keepdims=True)
    return centred * (factor * lax.rsqrt(spread + epsilon))


def half_silu(half):
    return half + half * jnp.tanh(half)


def dot(a, b):
    return jnp.dot(a, b, preferred_element_type=jnp.float32)


def dot_rows(a, b):
    return lax.dot_general(a, b, (((1,), (1,)), ((), ())), preferred_element_type=jnp.float32)


def lanes(head):
    return slice(head * HEAD_DIM, (head + 1) * HEAD_DIM)


def wide(columns, width):
    return jnp.concatenate([columns] * (width // columns.shape[1]), 1)


def places(top, bottom, left, right):
    shape = (bottom - top, right - left)
    row = top + lax.broadcasted_iota(jnp.int32, shape, 0)
    col = left + lax.broadcasted_iota(jnp.int32, shape, 1)
    return row, col


def local_blocks(low, high):
    edges = [low, *[e for e in range(0, high, BLOCK) if e > low], high]
    return list(zip(edges[:-1], edges[1:]))


class Cut:
    def __init__(self, micro, tok):
        self.micro, self.tok = micro, tok
        self.late = [tok // LATE_OTHER] * (micro - 1) + [tok // LATE_LAST]
        self.second_at = [sum(self.late[:m]) for m in range(micro)]
        self.first_at = [m * tok - sum(self.late[:m]) for m in range(micro)]
        self.second_rows = sum(self.late)
        self.first_rows = micro * tok - self.second_rows

    def rows(self, first, second, m, top, bottom):
        late = self.late[m]
        early = self.first_at[m] - late
        if top >= late:
            return first[early + top : early + bottom, :]
        low = self.second_at[m]
        if bottom <= late:
            return second[low + top : low + bottom, :]
        parts = [second[low + top : low + late, :], first[early + late : early + bottom, :]]
        return jnp.concatenate(parts, 0)


def cut_kernel(x, first, sems, *, cut):
    copies = []
    for m in range(cut.micro):
        rows = cut.tok - cut.late[m]
        source = x.at[m, pl.ds(cut.late[m], rows)]
        target = first.at[pl.ds(cut.first_at[m], rows)]
        copies.append(pltpu.make_async_copy(source, target, sems.at[m]))
    for copy in copies:
        copy.start()
    for copy in copies:
        copy.wait()


def stream_floors(spans, slot, block, live, tok):
    row = lax.broadcasted_iota(jnp.int32, (8, tok), 1)
    bound = jnp.int32(0)
    start = jnp.zeros((8, tok), jnp.int32)
    for k in range(spans.shape[1]):
        bound = bound + spans[slot, k]
        start = jnp.where(block * tok + row >= bound, bound, start)
    start = jnp.where(row < live, start - block * tok, FAR)
    return jnp.transpose(jnp.concatenate([start] * 16, 0))


def project_kernel(
    slot, first, x, w_in, lengths, valid,
    second, second_normed, gates, queries, keys, values, w_kv, own_floors, floors, counts,
    w_q, w_u, normed, spans, alive, sems,
    *, cut,
):
    micro, tok = cut.micro, cut.tok
    branch = w_q.shape[1]
    scale = 0.5 / math.sqrt(HEAD_DIM)
    block = lax.axis_index("seq")
    parts = {
        1: (w_kv.at[:, pl.ds(0, branch)], values),
        3: (w_kv.at[:, pl.ds(branch, branch)], keys),
        2: (w_q, queries),
        0: (w_u, gates),
    }
    small = [
        pltpu.make_async_copy(lengths, spans, sems.at[4]),
        pltpu.make_async_copy(valid, alive, sems.at[5]),
    ]
    seconds = [
        pltpu.make_async_copy(
            x.at[m, pl.ds(0, cut.late[m])],
            second.at[pl.ds(cut.second_at[m], cut.late[m])],
            sems.at[6 + m],
        )
        for m in range(micro)
    ]
    loads = {
        part: pltpu.make_async_copy(w_in.at[:, pl.ds(part * branch, branch)], there, sems.at[part])
        for part, (there, _) in parts.items()
    }
    queue = [*seconds, *small, *loads.values()]
    for copy in queue[:-3]:
        copy.start()

    def norm_rows(rows):
        return normalise(rows.astype(jnp.float32), norm_eps, 0.5).astype(jnp.bfloat16)

    for m in range(micro):
        for top in range(cut.late[m], tok, 128):
            rows = cut.rows(first, second, m, top, top + 128)
            normed[m * tok + top : m * tok + top + 128, :] = norm_rows(rows)
        if m == 0:
            queue[-3].start()
    for copy in queue[-2:]:
        copy.start()
    for copy in seconds:
        copy.wait()
    for m in range(micro):
        for top in range(0, cut.late[m], 128):
            rows = norm_rows(cut.rows(first, second, m, top, top + 128))
            normed[m * tok + top : m * tok + top + 128, :] = rows
            low = cut.second_at[m] + top
            second_normed[low : low + 128, :] = rows
    for copy in small:
        copy.wait()
    for number, (part, (weight, kept)) in enumerate(parts.items()):
        loads[part].wait()
        for m in range(micro):
            out = half_silu(dot(normed[m * tok : (m + 1) * tok, :], weight[...]))
            kept[m] = (out * scale if part == 2 else out).astype(jnp.bfloat16)
        if number == 0:
            row = lax.broadcasted_iota(jnp.int32, (tok, 128), 0)
            for m in range(micro):
                low = stream_floors(spans, slot + m, block, alive[slot + m, block], tok)
                own_floors[m] = low
                floors[m] = jnp.maximum(low + tok, row + 1)
                before = alive[slot + m, jnp.maximum(block - 1, 0)]
                counts[m] = jnp.full((8, 128), before, jnp.int32)


def own_kernel(queries, keys, values, own_floors, mixed):
    micro, tok, branch = queries.shape
    pending = []

    def finish(m, head, pieces):
        total = {}
        for (left, right), weights in pieces:
            product = dot(weights, values[m, left:right, lanes(head)])
            for top in range(left, tok, BLOCK):
                piece = product[top - left : top - left + BLOCK]
                total[top] = total[top] + piece if top in total else piece
        mixed[m, :, lanes(head)] = jnp.concatenate([total[t] for t in sorted(total)], 0)

    for m in range(micro):
        masks = {}
        for left, right in local_blocks(0, tok):
            row, col = places(left, tok, left, right)
            masks[left] = (col <= row) & (col >= wide(own_floors[m, left:tok], right - left))
        for head in range(branch // HEAD_DIM):
            pieces = []
            for left, right in local_blocks(0, tok):
                half = dot_rows(queries[m, left:tok, lanes(head)], keys[m, left:right, lanes(head)])
                weights = jnp.where(masks[left], half_silu(half), 0.0).astype(jnp.bfloat16)
                pieces.append(((left, right), weights))
            pending.append((m, head, pieces))
            if len(pending) > 1:
                finish(*pending.pop(0))
    finish(*pending.pop(0))


def far_rows(before, w_kv, keys, values, raw):
    branch = keys.shape[1]
    rows = before.shape[0]
    for top in range(0, rows, BLOCK):
        bottom = min(top + BLOCK, rows)
        normed = before[top:bottom, :]
        if raw:
            normed = normalise(normed.astype(jnp.float32), norm_eps, 0.5).astype(jnp.bfloat16)
        values[top:bottom, :] = half_silu(dot(normed, w_kv[:, :branch])).astype(jnp.bfloat16)
        keys[top:bottom, :] = half_silu(dot(normed, w_kv[:, branch:])).astype(jnp.bfloat16)


def far_sums(low, high, offset, queries, mixed, floors, counts, keys, values, m, at=None):
    blocks = local_blocks(low, high)[::-1]
    edges = sorted({0, *[e for b in blocks for e in b if e > 0]})
    masks = {}
    for left, right in blocks:
        _, col = places(0, right, left, right)
        reach = wide(jnp.concatenate([counts[m]] * (right // 8), 0), right - left)
        masks[left] = (col >= wide(floors[m, 0:right], right - left)) & (col < reach)
    sums = []
    pending = []

    def finish(head, pieces):
        total = {}
        for top, bottom in zip(edges, edges[1:]):
            where = (m, slice(top, bottom)) if at is None else (slice(at + top, at + bottom),)
            total[top] = mixed[(*where, lanes(head))]
        for (left, right), weights in pieces:
            product = dot(weights, values[offset + left : offset + right, lanes(head)])
            for top, bottom in zip(edges, edges[1:]):
                if bottom <= right:
                    total[top] = total[top] + product[top:bottom]
        sums.append(jnp.concatenate([total[t] for t in sorted(total)], 0))

    for head in range(queries.shape[2] // HEAD_DIM):
        pieces = []
        for left, right in blocks:
            half = dot_rows(
                queries[m, 0:right, lanes(head)],
                keys[offset + left : offset + right, lanes(head)],
            )
            weights = jnp.where(masks[left], half_silu(half), 0.0).astype(jnp.bfloat16)
            pieces.append(((left, right), weights))
        pending.append((head, pieces))
        if len(pending) > 1:
            finish(*pending.pop(0))
    finish(*pending.pop(0))
    return sums


def close(sums, top, bottom, x_rows, w_out, gates, m, keep):
    for low in range(top, bottom, BLOCK):
        high = min(low + BLOCK, bottom)
        attended = jnp.concatenate([s[low:high] for s in sums], 1)
        attended = normalise(attended, out_eps * WINDOW)
        gated = (attended * gates[m, low:high, :].astype(jnp.float32)).astype(jnp.bfloat16)
        result = x_rows(m, low, high).astype(jnp.float32) + dot(gated, w_out[...])
        keep(m, low, high, result.astype(jnp.bfloat16))


def far_first_kernel(
    before, first, second, w_kv, w_out, gates, queries, mixed, floors, counts,
    done, rest, keys, values, *, cut,
):
    def keep(m, low, high, result):
        shift = cut.first_at[m] - cut.late[m]
        done[shift + low : shift + high, :] = result

    x_rows = functools.partial(cut.rows, first, second)
    far_rows(before, w_kv, keys, values, True)
    for m in range(cut.micro):
        late = cut.late[m]
        sums = far_sums(
            late, cut.tok, cut.first_at[m] - late, queries, mixed, floors, counts, keys, values, m
        )
        low = cut.second_at[m]
        for head, total in enumerate(sums):
            rest[low : low + late, lanes(head)] = total[:late]
        close(sums, late, cut.tok, x_rows, w_out, gates, m, keep)


def far_second_kernel(
    before, second, w_kv, w_out, gates, queries, rest, floors, counts, first_done,
    out, keys, values, done, sems, *, cut,
):
    copies = []

    def send(source, m, low, high):
        there = out.at[0, m, pl.ds(low, high - low)]
        copies.append(pltpu.make_async_copy(source, there, sems.at[len(copies)]))
        copies[-1].start()

    for m in range(cut.micro):
        rows = cut.tok - cut.late[m]
        send(first_done.at[pl.ds(cut.first_at[m], rows)], m, cut.late[m], cut.tok)

    def keep(m, low, high, result):
        at = cut.second_at[m]
        done[at + low : at + high, :] = result
        send(done.at[pl.ds(at + low, high - low)], m, low, high)

    far_rows(before, w_kv, keys, values, False)
    x_rows = functools.partial(cut.rows, None, second)
    for m in range(cut.micro):
        at = cut.second_at[m]
        sums = far_sums(
            0, cut.late[m], at, queries, rest, floors, counts, keys, values, m, at
        )
        close(sums, 0, cut.late[m], x_rows, w_out, gates, m, keep)
    for copy in copies:
        copy.wait()


VMEM = pl.BlockSpec(memory_space=pltpu.VMEM)
SMEM = pl.BlockSpec(memory_space=pltpu.SMEM)
HBM = pl.BlockSpec(memory_space=pltpu.HBM)


def kept_in_hbm(x):
    return pltpu.with_memory_space_constraint(x, pltpu.HBM)


def layer(x, w_in, w_out, lengths, valid, slot):
    micro, tok, width = x.shape
    branch = w_out.shape[0]
    cut = Cut(micro, tok)
    early, late = cut.first_rows, cut.second_rows
    bf16, f32, i32 = jnp.bfloat16, jnp.float32, jnp.int32
    shape = jax.ShapeDtypeStruct
    params = pltpu.CompilerParams(vmem_limit_bytes=24 << 20)

    def cost(rows, flops, tanhs):
        return pl.CostEstimate(
            flops=rows * flops, transcendentals=rows * tanhs, bytes_accessed=4 << 20
        )

    x = kept_in_hbm(x)
    first = pl.pallas_call(
        functools.partial(cut_kernel, cut=cut),
        out_shape=shape((early, width), bf16),
        in_specs=[HBM],
        out_specs=VMEM,
        scratch_shapes=[pltpu.SemaphoreType.DMA((micro,))],
        compiler_params=params,
        name="cut",
    )(x)
    first_come = shifted(first, "seq", 1)
    fixed = isinstance(slot, int)
    wide_rows = shape((micro, tok, branch), bf16)
    second, second_normed, gates, queries, keys, values, w_kv, own_floors, floors, counts = (
        pl.pallas_call(
            functools.partial(project_kernel, slot, cut=cut)
            if fixed
            else functools.partial(project_kernel_at, cut=cut),
            out_shape=(
                shape((late, width), bf16),
                shape((late, width), bf16),
                *[wide_rows] * 4,
                shape((width, 2 * branch), bf16),
                shape((micro, tok, 128), i32),
                shape((micro, tok, 128), i32),
                shape((micro, 8, 128), i32),
            ),
            in_specs=([] if fixed else [SMEM]) + [VMEM, HBM, HBM, HBM, HBM],
            out_specs=(VMEM,) * 10,
            scratch_shapes=[
                pltpu.VMEM((width, branch), bf16),
                pltpu.VMEM((width, branch), bf16),
                pltpu.VMEM((micro * tok, width), bf16),
                pltpu.SMEM(lengths.shape, i32),
                pltpu.SMEM(valid.shape, i32),
                pltpu.SemaphoreType.DMA((6 + micro,)),
            ],
            compiler_params=params,
            cost_estimate=cost(micro * tok, branch * 8 * width, branch * 4),
            name="project",
        )(*([] if fixed else [slot[None]]), first, x, *map(kept_in_hbm, (w_in, lengths, valid)))
    )
    second_come = shifted(second_normed, "seq", 1)
    mixed = pl.pallas_call(
        own_kernel,
        out_shape=shape((micro, tok, branch), f32),
        in_specs=[VMEM] * 4,
        out_specs=VMEM,
        compiler_params=params,
        cost_estimate=cost(micro * tok, branch * 4 * tok, branch * 2),
        name="own",
    )(queries, keys, values, own_floors)
    first_done, rest = pl.pallas_call(
        functools.partial(far_first_kernel, cut=cut),
        out_shape=(shape((early, width), bf16), shape((late, branch), f32)),
        in_specs=[VMEM] * 10,
        out_specs=(VMEM, VMEM),
        scratch_shapes=[pltpu.VMEM((early, branch), bf16)] * 2,
        compiler_params=params,
        cost_estimate=cost(early, branch * (6 * width + 4 * tok), branch * 4),
        name="far_first",
    )(first_come, first, second, w_kv, w_out, gates, queries, mixed, floors, counts)
    return pl.pallas_call(
        functools.partial(far_second_kernel, cut=cut),
        out_shape=shape((1, micro, tok, width), bf16),
        in_specs=[VMEM] * 10,
        out_specs=HBM,
        scratch_shapes=[
            *[pltpu.VMEM((late, branch), bf16)] * 2,
            pltpu.VMEM((late, width), bf16),
            pltpu.SemaphoreType.DMA((micro * (2 + tok // BLOCK),)),
        ],
        compiler_params=params,
        cost_estimate=cost(late, branch * (6 * width + 4 * tok), branch * 4),
        name="far_second",
    )(second_come, second, w_kv, w_out, gates, queries, rest, floors, counts, first_done)[0]


def project_kernel_at(slot, *refs, cut):
    project_kernel(slot[0], *refs, cut=cut)


def shards(inputs, w_in, w_out, lengths, valid):
    micro, tok, width = inputs.shape
    sections = lax.axis_size("pipe")
    if sections == 1:
        return layer(inputs, w_in[0], w_out[0], lengths, valid, 0)[None]
    section = lax.axis_index("pipe")

    def tick(step, carry):
        incoming, states = carry
        slot = step - section
        active = (slot >= 0) & (slot < micro)
        index = jnp.clip(slot, 0, micro - 1)
        fresh = lax.dynamic_index_in_dim(inputs, index, 0, keepdims=False)
        x_rows = jnp.where(section == 0, fresh, incoming)
        result = layer(x_rows[None], w_in[0], w_out[0], lengths, valid, index)[0]
        updated = lax.dynamic_update_slice(
            states, result[None, None], (jnp.int32(0), index, jnp.int32(0), jnp.int32(0))
        )
        states = jnp.where(active, updated, states)
        return (shifted(result, "pipe", 1), states)

    start_states = jnp.zeros((1, micro, tok, width), jnp.bfloat16)
    start_rows = jnp.zeros((tok, width), jnp.bfloat16)
    _, states = lax.fori_loop(0, sections + micro - 1, tick, (start_rows, start_states))
    return states


def solution(mesh):
    in_specs = (P(None, "seq", None), P("pipe", None, None), P("pipe", None, None), P(), P())
    out_specs = P("pipe", None, "seq", None)
    return jax.shard_map(shards, mesh=mesh, in_specs=in_specs, out_specs=out_specs, check_vma=False)
```

time: 22.1 us -> 22 us (level)
  the two profiles are of different devices: /device:TPU:0 before, /device:TPU:24 now
where the time goes in v4:
time: 22 us; the launch traced here: 21.9 us
  Pallas kernels  13.7 us (62%)
  starting transfers between devices  5.43 us (25%)
  waiting for transfers between devices  2.69 us (12%)
    ppermute x2, starting transfers between devices, shifted(): return lax.ppermute(x, axis, pairs)  5.43 us
    pallas_call x1, Pallas kernels, layer(): pl.pallas_call(functools.partial(project_kernel, slot, cut=cut) if fixed...  4.39 us
    pallas_call x1, Pallas kernels, layer(): pl.pallas_call(functools.partial(far_first_kernel, cut=cut), out_shape=(s...  3.46 us
    pallas_call x1, Pallas kernels, layer(): pl.pallas_call(functools.partial(far_second_kernel, cut=cut), out_shape=s...  2.85 us
    ppermute x2, waiting for transfers between devices, shifted(): return lax.ppermute(x, axis, pairs)  2.69 us
    pallas_call x1, Pallas kernels, layer(): pl.pallas_call(own_kernel, out_shape=shape((micro, tok, branch), f32), in...  1.9 us
    pallas_call x1, Pallas kernels, layer(): pl.pallas_call(functools.partial(cut_kernel, cut=cut), out_shape=shape((e...  1.08 us
  transfers between devices with their start and end apart: 2, of which 2 were waited for; matrix products, arithmetic and copies ran while one was open for 0% of the time, Pallas kernels for 45%

profile of v4, /device:TPU:24, one launch (start us, length us, event | category | flops | bytes accessed | tf_op | source)
XLA Modules:
  0.0 21.9 jit_solution(2732756976017827920)
XLA Ops:
  0.0 1.1 %cut.1.first = bf16[640,512]{1,0:T(8,128)(2,1)S(1)} custom-call(bf16[2,512,512]{2,1,0:T(8,128)(2,1)} %x.3), custom_call_target="tpu_custom_call" | custom-call | tf_op jit(solution)/shard_map/cut/pallas_call | solution.py:353
  1.1 1.9 %collective-permute-start.1 = (bf16[640,512]{1,0:T(8,128)(2,1)S(1)}, bf16[640,512]{1,0:T(8,128)(2,1)S(1)}, u32[]{:S(2)}, u32[]{:S(2)}) collective-permute-start(bf16[640,512]{1,0:T(8,128)(2,1)S(1)} %cut.1.first), channel_id=1, source_target_pairs={{0,1},{1,2},{2,3},{3,4},{4,5},{5,6},{6,7},{7,8},{8,9},{9,10},{10,1... | collective-permute-start | bytes 1966088 | tf_op jit(solution)/shard_map/ppermute | solution.py:26
  3.0 4.4 %project.1 = (bf16[384,512]{1,0:T(8,128)(2,1)S(1)}, bf16[384,512]{1,0:T(8,128)(2,1)S(1)}, bf16[2,512,512]{2,1,0:T(8,128)(2,1)S(1)}, bf16[2,512,512]{2,1,0:T(8,12...) custom-call(bf16[640,512]{1,0:T(8,128)(2,1)S(1)} %cut.1.first, ...), custom_call_target="tpu_custom_call" | custom-call | flops 2147483648 | bytes 4194304 | tf_op jit(solution)/shard_map/project/pallas_call | solution.py:366
  7.4 3.5 %collective-permute-start = (bf16[384,512]{1,0:T(8,128)(2,1)S(1)}, bf16[384,512]{1,0:T(8,128)(2,1)S(1)}, u32[]{:S(2)}, u32[]{:S(2)}) collective-permute-start(bf16[384,512]{1,0:T(8,128)(2,1)S(1)} %get-tuple-element.17), channel_id=1, source_target_pairs={{0,1},{1,2},{2,3},{3,4},{4,5},{5,6},{6,7},{7,8},{8,9},{9,10},{10,1... | collective-permute-start | bytes 1179656 | tf_op jit(solution)/shard_map/ppermute | solution.py:26
  10.9 0.0 copy-start
  10.9 1.9 %own.1.mixed = f32[2,512,512]{2,1,0:T(8,128)S(1)} custom-call(bf16[2,512,512]{2,1,0:T(8,128)(2,1)S(1)} %get-tuple-element.21.queries, bf16[2,512,512]{2,1,0:T(8,128)(2,1)S(1)} %get-tuple-element.22.keys, bf16[2,512,512]{2,1,0:T(8,128)(2,1)S(1)} %get-tuple-element.23.values, s32[2,512,128]{2,1,0:T(8,128)S(1)} %get-tuple-element.24.own_floors), custom_call_target="tpu_custom_call" | custom-call | flops 1073741824 | bytes 4194304 | tf_op jit(solution)/shard_map/own/pallas_call | solution.py:395
  12.8 1.9 %collective-permute-done.1.before = bf16[640,512]{1,0:T(8,128)(2,1)S(1)} collective-permute-done((bf16[640,512]{1,0:T(8,128)(2,1)S(1)}, bf16[640,512]{1,0:T(8,128)(2,1)S(1)}, u32[]{:S(2)}, u32[]{:S(2)}) %collective-permute-start.1) | collective-permute-done | bytes 655392 | tf_op jit(solution)/shard_map/ppermute | solution.py:26
  14.8 0.0 copy-done
  14.8 3.5 %far_first.1 = (bf16[640,512]{1,0:T(8,128)(2,1)S(1)}, f32[384,512]{1,0:T(8,128)S(1)}) custom-call(bf16[640,512]{1,0:T(8,128)(2,1)S(1)} %collective-permute-done.1.before, bf16[640,512]{1,0:T(8,128)(2,1)S(1)} %cut.1.first, bf16[384,512]{1,0:T(8,128)(2,1)S(1)} %get-tuple-element.18.second, bf16[512,1024]{1,0:T(8,128)(2,1)S(1)} %get-tuple-element.19.w_kv, ...), custom_call_target="tpu_custom_call" | custom-call | flops 1677721600 | bytes 4194304 | tf_op jit(solution)/shard_map/far_first/pallas_call | solution.py:404
  18.3 0.7 %collective-permute-done.before = bf16[384,512]{1,0:T(8,128)(2,1)S(1)} collective-permute-done((bf16[384,512]{1,0:T(8,128)(2,1)S(1)}, bf16[384,512]{1,0:T(8,128)(2,1)S(1)}, u32[]{:S(2)}, u32[]{:S(2)}) %collective-permute-start) | collective-permute-done | bytes 393248 | tf_op jit(solution)/shard_map/ppermute | solution.py:26
  19.0 2.9 %far_second.1 = bf16[1,2,512,512]{3,2,1,0:T(8,128)(2,1)} custom-call(bf16[384,512]{1,0:T(8,128)(2,1)S(1)} %collective-permute-done.before, bf16[384,512]{1,0:T(8,128)(2,1)S(1)} %get-tuple-element.18.second, bf16[512,1024]{1,0:T(8,128)(2,1)S(1)} %get-tuple-element.19.w_kv, bf16[512,512]{1,0:T(8,128)(2,1)S(1)} %bitcast.3, ...), custom_call_target="tpu_custom_call" | custom-call | flops 1006632960 | bytes 4194304 | tf_op jit(solution)/shard_map/far_second/pallas_call | solution.py:414
Async XLA Ops:
  1.1 13.7 %collective-permute-start.1 = (bf16[640,512]{1,0:T(8,128)(2,1)S(1)}, bf16[640,512]{1,0:T(8,128)(2,1)S(1)}, u32[]{:S(2)}, u32[]{:S(2)}) collective-permute-start(bf16[640,512]{1,0:T(8,128)(2,1)S(1)} %cut.1.first), channel_id=1, source_target_pairs={{0,1},{1,2},{2,3},{3,4},{4,5},{5,6},{6,7},{7,8},{8,9},{9,10},{10,1... | collective-permute-start | bytes 1966088 | tf_op jit(solution)/shard_map/ppermute | solution.py:26
  7.4 11.6 %collective-permute-start = (bf16[384,512]{1,0:T(8,128)(2,1)S(1)}, bf16[384,512]{1,0:T(8,128)(2,1)S(1)}, u32[]{:S(2)}, u32[]{:S(2)}) collective-permute-start(bf16[384,512]{1,0:T(8,128)(2,1)S(1)} %get-tuple-element.17), channel_id=1, source_target_pairs={{0,1},{1,2},{2,3},{3,4},{4,5},{5,6},{6,7},{7,8},{8,9},{9,10},{10,1... | collective-permute-start | bytes 1179656 | tf_op jit(solution)/shard_map/ppermute | solution.py:26
  10.9 3.9 %copy-start = (bf16[1,512,512]{2,1,0:T(8,128)(2,1)S(1)}, bf16[1,512,512]{2,1,0:T(8,128)(2,1)}, u32[]{:S(2)}) copy-start(bf16[1,512,512]{2,1,0:T(8,128)(2,1)} %param.7) | copy-start | bytes 1572868
